TPU v7x, 64 devices: a 2x2x8 block of a 4x4x8 slice. The times are simulated.
64 devices in a mesh: rep: 8 (over x, y, core), dp: 8 (over z).
Axes of the slice: x: 2, y: 2, z: 8, core: 2. Of those that a mesh axis runs over, the one named last changes fastest.
The devices are a block of a 4x4x8 slice.
Arguments:
- g_w_gate: bfloat16 [64, 2, 512, 1408], P(('rep', 'dp')), parts along dimension 0
- g_w_up: bfloat16 [64, 2, 512, 1408], P(('rep', 'dp')), parts along dimension 0
- g_w_down: bfloat16 [64, 2, 1408, 512], P(('rep', 'dp')), parts along dimension 0
- w_gate: bfloat16 [2, 512, 1408], replicated
- w_up: bfloat16 [2, 512, 1408], replicated
- w_down: bfloat16 [2, 1408, 512], replicated
- m_w_gate: float32 [2, 512, 1408], P(None, 'dp')
- m_w_up: float32 [2, 512, 1408], P(None, 'dp')
- m_w_down: float32 [2, 1408, 512], P(None, 'dp')
- v_w_gate: float32 [2, 512, 1408], P(None, 'dp')
- v_w_up: float32 [2, 512, 1408], P(None, 'dp')
- v_w_down: float32 [2, 1408, 512], P(None, 'dp')
Outputs:
- output 1: bfloat16 [16, 512, 1408], P('rep'), parts along dimension 0
- output 2: bfloat16 [16, 512, 1408], P('rep'), parts along dimension 0
- output 3: bfloat16 [16, 1408, 512], P('rep'), parts along dimension 0
- output 4: float32 [16, 512, 1408], P('rep', 'dp'), parts along dimension 0
- output 5: float32 [16, 512, 1408], P('rep', 'dp'), parts along dimension 0
- output 6: float32 [16, 1408, 512], P('rep', 'dp'), parts along dimension 0
- output 7: float32 [16, 512, 1408], P('rep', 'dp'), parts along dimension 0
- output 8: float32 [16, 512, 1408], P('rep', 'dp'), parts along dimension 0
- output 9: float32 [16, 1408, 512], P('rep', 'dp'), parts along dimension 0
There are 8 independent parts. A program takes and returns all parts, laid end to end along the dimension named above; an argument that names none is the same for every part.
All inputs are finite; a program needn't handle non-finite values.
Results may differ from a plain program's by a relative error of at most 0.022.
Values are sent between devices in bfloat16 or wider.
A program may use at most 768 MiB of HBM per device.

v0:
```python
import jax
import jax.numpy as jnp
from jax import lax
from jax.sharding import PartitionSpec as P


def adamw(w, m, v, g):
    m = 0.9 * m + 0.1 * g
    v = 0.95 * v + 0.05 * g * g
    step = m * lax.rsqrt(v + 1e-8) + 0.1 * w
    return (w - 0.02 * step).astype(jnp.bfloat16), m, v


def solution(mesh):
    def step(*arrays):
        terms, weights, m, v = (arrays[i : i + 3] for i in (0, 3, 6, 9))
        gradients = [lax.psum_scatter(t[0], "dp", scatter_dimension=1, tiled=True).astype(jnp.float32) for t in terms]
        me = lax.axis_index("dp")
        own = [lax.dynamic_slice_in_dim(w, me * one.shape[1], one.shape[1], 1).astype(jnp.float32) for w, one in zip(weights, m, strict=True)]
        new = [adamw(w, m, v, g) for w, m, v, g in zip(own, m, v, gradients, strict=True)]
        whole = [lax.all_gather(one[0], "dp", axis=1, tiled=True) for one in new]
        return (*whole, *(one[1] for one in new), *(one[2] for one in new))

    all_of, cut = P(None, None, None), P(None, "dp", None)
    return jax.shard_map(
        step,
        mesh=mesh,
        in_specs=(P(("rep", "dp"), None, None, None),) * 3 + (all_of,) * 3 + (cut,) * 6,
        out_specs=(P("rep", None, None),) * 3 + (P("rep", "dp", None),) * 6,
        check_vma=False,
    )
```

profile of v0, /device:TPU:22, one launch (start us, length us, event | category | flops | bytes accessed | tf_op | source)
XLA Modules:
  0.0 282.0 jit_solution(8375374704700163050)
XLA Ops:
  7.2 0.1 reduce-scatter.8.cloned.1.call-start
  7.3 0.7 reduce-scatter.8.cloned.1.call-update
  8.0 0.1 reduce-scatter.6.cloned.1.call-start
  8.1 0.0 copy-start.2
  8.1 0.0 copy-start.3
  8.1 0.7 reduce-scatter.6.cloned.1.call-update
  8.8 0.1 reduce-scatter.4.cloned.1.call-start
  8.9 0.7 reduce-scatter.4.cloned.1.call-update
  9.6 0.0 copy-start.4
  9.6 0.0 copy-start.5
  9.6 0.1 all-gather.8.cloned.1.call-start
  9.7 46.4 %reduce-scatter.8.cloned.1.call-done = bf16[2,176,512]{2,1,0:T(8,128)(2,1)} async-done(((bf16[2,1408,512]{2,1,0:T(8,128)(2,1)}), bf16[2,176,512]{2,1,0:T(8,128)(2,1)}) %reduce-scatter.8.cloned.1.call-update) | async-done | bytes 360464 | tf_op jit(solution)/shard_map/reduce_scatter | solution.py:17
  56.1 0.0 copy-done.2
  56.1 0.0 copy-done.3
  56.1 2.5 fusion.10
  58.6 0.0 copy-start.6
  58.6 0.0 copy-start.7
  58.6 0.1 all-gather.8.cloned.1.call-update
  58.7 0.1 all-gather.6.cloned.1.call-start
  58.8 41.3 %reduce-scatter.6.cloned.1.call-done = bf16[2,64,1408]{2,1,0:T(8,128)(2,1)} async-done(((bf16[2,512,1408]{2,1,0:T(8,128)(2,1)}), bf16[2,64,1408]{2,1,0:T(8,128)(2,1)}) %reduce-scatter.6.cloned.1.call-update) | async-done | bytes 360464 | tf_op jit(solution)/shard_map/reduce_scatter | solution.py:17
  100.0 0.0 copy-done.4
  100.0 0.0 copy-done.5
  100.0 2.5 fusion.6
  102.5 0.1 all-gather.6.cloned.1.call-update
  102.6 0.1 all-gather.4.cloned.1.call-start
  102.7 41.3 %reduce-scatter.4.cloned.1.call-done = bf16[2,64,1408]{2,1,0:T(8,128)(2,1)} async-done(((bf16[2,512,1408]{2,1,0:T(8,128)(2,1)}), bf16[2,64,1408]{2,1,0:T(8,128)(2,1)}) %reduce-scatter.4.cloned.1.call-update) | async-done | bytes 360464 | tf_op jit(solution)/shard_map/reduce_scatter | solution.py:17
  144.0 0.0 copy-done.6
  144.0 0.0 copy-done.7
  144.0 2.5 fusion.2
  146.5 0.1 all-gather.4.cloned.1.call-update
  146.5 39.3 %all-gather.8.cloned.1.call-done = bf16[2,1408,512]{2,1,0:T(8,128)(2,1)} async-done(((bf16[2,176,512]{2,1,0:T(8,128)(2,1)}), bf16[2,1408,512]{2,1,0:T(8,128)(2,1)}) %all-gather.8.cloned.1.call-update) | async-done | bytes 2883600 | tf_op jit(solution)/shard_map/all_gather | solution.py:21
  185.8 40.5 %all-gather.6.cloned.1.call-done = bf16[2,512,1408]{2,1,0:T(8,128)(2,1)} async-done(((bf16[2,64,1408]{2,1,0:T(8,128)(2,1)}), bf16[2,512,1408]{2,1,0:T(8,128)(2,1)}) %all-gather.6.cloned.1.call-update) | async-done | bytes 2883600 | tf_op jit(solution)/shard_map/all_gather | solution.py:21
  226.3 40.6 %all-gather.4.cloned.1.call-done = bf16[2,512,1408]{2,1,0:T(8,128)(2,1)} async-done(((bf16[2,64,1408]{2,1,0:T(8,128)(2,1)}), bf16[2,512,1408]{2,1,0:T(8,128)(2,1)}) %all-gather.4.cloned.1.call-update) | async-done | bytes 2883600 | tf_op jit(solution)/shard_map/all_gather | solution.py:21
  266.9 0.0 copy-start.1
  266.9 3.8 %copy.24 = bf16[2,512,1408]{2,1,0:T(8,128)(2,1)} copy(bf16[2,512,1408]{2,1,0:T(8,128)(2,1)} %all-gather.4.cloned.1.call-done) | data formatting | bytes 5767168
  270.7 0.0 copy-done.1
  270.7 0.0 copy-start
  270.7 1.6 copy.25
  272.2 1.3 copy-done
  273.5 1.6 copy.26
Async XLA Ops:
  7.2 48.9 %reduce-scatter.8.cloned.1.call-start = ((), (), s32[]{:S(2)}) async-start(), calls=%async_computation.7 | async-start | bytes 3244032 | tf_op jit(solution)/shard_map/reduce_scatter | solution.py:17
  8.0 92.1 %reduce-scatter.6.cloned.1.call-start = ((), (), s32[]{:S(2)}) async-start(), calls=%async_computation.5 | async-start | bytes 3244032 | tf_op jit(solution)/shard_map/reduce_scatter | solution.py:17
  8.1 48.1 %copy-start.2 = (f32[2,176,512]{2,1,0:T(8,128)S(1)}, f32[2,176,512]{2,1,0:T(8,128)}, u32[]{:S(2)}) copy-start(f32[2,176,512]{2,1,0:T(8,128)} %param.23) | copy-start | bytes 2162692
  8.1 48.0 %copy-start.3 = (f32[2,176,512]{2,1,0:T(8,128)S(1)}, f32[2,176,512]{2,1,0:T(8,128)}, u32[]{:S(2)}) copy-start(f32[2,176,512]{2,1,0:T(8,128)} %param.20) | copy-start | bytes 2162692
  8.8 135.2 %reduce-scatter.4.cloned.1.call-start = ((), (), s32[]{:S(2)}) async-start(), calls=%async_computation.3 | async-start | bytes 3244032 | tf_op jit(solution)/shard_map/reduce_scatter | solution.py:17
  9.6 90.5 %copy-start.4 = (f32[2,64,1408]{2,1,0:T(8,128)S(1)}, f32[2,64,1408]{2,1,0:T(8,128)}, u32[]{:S(2)}) copy-start(f32[2,64,1408]{2,1,0:T(8,128)} %param.22) | copy-start | bytes 2162692
  9.6 90.4 %copy-start.5 = (f32[2,64,1408]{2,1,0:T(8,128)S(1)}, f32[2,64,1408]{2,1,0:T(8,128)}, u32[]{:S(2)}) copy-start(f32[2,64,1408]{2,1,0:T(8,128)} %param.19) | copy-start | bytes 2162692
  9.6 176.2 %all-gather.8.cloned.1.call-start = ((), (), s32[]{:S(2)}) async-start(), calls=%async_computation.8 | async-start | bytes 3244032 | tf_op jit(solution)/shard_map/all_gather | solution.py:21
  58.6 85.4 %copy-start.6 = (f32[2,64,1408]{2,1,0:T(8,128)S(1)}, f32[2,64,1408]{2,1,0:T(8,128)}, u32[]{:S(2)}) copy-start(f32[2,64,1408]{2,1,0:T(8,128)} %param.21) | copy-start | bytes 2162692
  58.6 85.4 %copy-start.7 = (f32[2,64,1408]{2,1,0:T(8,128)S(1)}, f32[2,64,1408]{2,1,0:T(8,128)}, u32[]{:S(2)}) copy-start(f32[2,64,1408]{2,1,0:T(8,128)} %param.18) | copy-start | bytes 2162692
  58.7 167.7 %all-gather.6.cloned.1.call-start = ((), (), s32[]{:S(2)}) async-start(), calls=%async_computation.6 | async-start | bytes 3244032 | tf_op jit(solution)/shard_map/all_gather | solution.py:21
  102.6 164.3 %all-gather.4.cloned.1.call-start = ((), (), s32[]{:S(2)}) async-start(), calls=%async_computation.4 | async-start | bytes 3244032 | tf_op jit(solution)/shard_map/all_gather | solution.py:21
  266.9 3.8 %copy-start.1 = (bf16[2,512,1408]{2,1,0:T(8,128)(2,1)S(1)}, bf16[2,512,1408]{2,1,0:T(8,128)(2,1)}, u32[]{:S(2)}) copy-start(bf16[2,512,1408]{2,1,0:T(8,128)(2,1)} %all-gather.6.cloned.1.call-done) | copy-start | bytes 8650756
  270.7 2.9 %copy-start = (bf16[2,1408,512]{2,1,0:T(8,128)(2,1)S(1)}, bf16[2,1408,512]{2,1,0:T(8,128)(2,1)}, u32[]{:S(2)}) copy-start(bf16[2,1408,512]{2,1,0:T(8,128)(2,1)} %all-gather.8.cloned.1.call-done) | copy-start | bytes 8650756
Sparse Core Ops, SparseCore 0:
  10.4 45.6 reduce-scatter.7
  58.5 41.5 reduce-scatter.5
  102.4 41.5 reduce-scatter.3
  146.0 39.7 all-gather.7
  187.8 38.4 all-gather.5
  228.4 38.4 all-gather.3
where the time goes:
time: 282 us
  waiting for transfers between devices  252 us (89%)
  between operations  14.2 us (5%)
  local copies, waits for them, and re-layouts  8.22 us (3%)
  other arithmetic  7.47 us (3%)
    reduce_scatter x3, waiting for transfers between devices, step(): lax.psum_scatter(t[0], 'dp', scatter_dimension=1, tiled=True)  129 us
    all_gather x3, waiting for transfers between devices, step(): whole = [lax.all_gather(one[0], 'dp', axis=1, tiled=True) for one in new]  120 us
    unnamed x19, local copies, waits for them, and re-layouts  8.22 us
    convert_element_type x3, other arithmetic, adamw(): return ((w - 0.02 * step).astype(jnp.bfloat16), m, v)  7.47 us
  transfers between devices with their start and end apart: 6, of which 6 were waited for; matrix products, arithmetic and copies ran while one was open for 3% of the time, Pallas kernels for 0%

commit v1 on v0

v1 whole, which is shorter than its diff:
```python
import functools

import jax
import jax.numpy as jnp
from jax import lax
from jax.experimental import pallas as pl
from jax.experimental.pallas import tpu as pltpu
from jax.sharding import PartitionSpec as P

MESH = pl.DeviceIdType.MESH
ROWS = 16
VMEM = 54_000_000


def adamw(w, m, v, g):
    m = 0.9 * m + 0.1 * g
    v = 0.95 * v + 0.05 * g * g
    step = m * lax.rsqrt(v + 1e-8) + 0.1 * w
    return (w - 0.02 * step).astype(jnp.bfloat16), m, v


class Plan:
    def __init__(self, n, pieces):
        self.n, self.pieces = n, pieces
        far, near = n // 2, (n - 1) // 2
        self.hops = [(far, near) if p % 2 == 0 else (near, far) for p in range(pieces)]
        self.far = far

    def order(self, side, hops_left):
        live = [p for p in range(self.pieces) if self.hops[p][side] >= hops_left]
        if hops_left == self.far - 1:
            live.sort(key=lambda p: self.hops[p][side])
        return live

    def spread(self, side, hop):
        live = [p for p in range(self.pieces) if self.hops[p][side] >= hop]
        if hop == self.far - 1:
            live.sort(key=lambda p: -self.hops[p][side])
        return live


def kernel(plan, kinds, names, *refs):
    n, pieces = plan.n, plan.pieces
    weights = len(names)
    g, w, m, v = (refs[i * weights : (i + 1) * weights] for i in range(4))
    w_out, m_out, v_out = (refs[(4 + i) * weights : (5 + i) * weights] for i in range(3))
    rest = list(refs[7 * weights :])
    terms, inbox, own, m_in, v_in = (rest[i * len(kinds) : (i + 1) * len(kinds)] for i in range(5))
    load_sem, state_sem, send_sem, recv_sem, gather_send_sem, gather_recv_sem = rest[5 * len(kinds) :]

    me = lax.axis_index("dp")
    to = [lax.rem(me + 1, n), lax.rem(me + n - 1, n)]
    at = lambda away: lax.rem(me + (away + n), n)

    layers = w[0].shape[0]
    where = []
    for p in range(pieces):
        k, layer = p // layers, p % layers
        kind, first = names[k]
        where.append((k, layer, kind, first * layers + layer))

    def rows(p, owner):
        r = m[where[p][0]].shape[1]
        return pl.ds(pl.multiple_of(owner * r, r), r)

    def signed(side, hops):
        return hops if side == 0 else -hops

    def term(p, away):
        _, _, kind, place = where[p]
        return terms[kind].at[place, away % n]

    def slot(p, side, hops_left):
        _, _, kind, place = where[p]
        return inbox[kind].at[place, side * plan.far + hops_left - 1]

    def load(p, away):
        k, layer, _, _ = where[p]
        return pltpu.make_async_copy(g[k].at[0, layer, rows(p, at(away))], term(p, away), load_sem.at[p, away % n])

    def state_loads(k):
        kind, first = names[k]
        mine = pl.ds(first * layers, layers)
        block = rows(k * layers, me)
        return [
            pltpu.make_async_copy(w[k].at[:, block], own[kind].at[mine], state_sem.at[k, 0]),
            pltpu.make_async_copy(m[k], m_in[kind].at[mine], state_sem.at[k, 1]),
            pltpu.make_async_copy(v[k], v_in[kind].at[mine], state_sem.at[k, 2]),
        ]

    loads = {}
    first_wave = [(p, s, plan.hops[p][s]) for h in (plan.far, plan.far - 1) for p in range(pieces) for s in (0, 1) if plan.hops[p][s] == h]
    wanted = [(p, signed(s, h)) for p, s, h in first_wave]
    for h in range(plan.far - 1, 0, -1):
        wanted += [(p, signed(s, h)) for p in range(pieces) for s in (0, 1)]
    wanted += [(p, 0) for p in range(pieces)]
    for p, away in wanted:
        if (p, away % n) not in loads:
            loads[p, away % n] = load(p, away)
            loads[p, away % n].start()
    states = [state_loads(k) for k in range(weights)]
    for copies in states:
        for copy in copies:
            copy.start()

    barrier = pltpu.get_barrier_semaphore()
    for neighbour in to:
        pl.semaphore_signal(barrier, inc=1, device_id={"dp": neighbour}, device_id_type=MESH)
    pl.semaphore_wait(barrier, 2)

    def reduce_copy(p, side, hops_left):
        return pltpu.make_async_remote_copy(
            src_ref=term(p, signed(side, hops_left)),
            dst_ref=slot(p, side, hops_left),
            send_sem=send_sem.at[p, side, hops_left - 1],
            recv_sem=recv_sem.at[p, side, hops_left - 1],
            device_id={"dp": to[side]},
            device_id_type=MESH,
        )

    def by_rows(ref, body):
        lax.fori_loop(0, ref.shape[0] // ROWS, lambda i, _: body(pl.ds(pl.multiple_of(i * ROWS, ROWS), ROWS)), None)

    def add(into, other):
        def body(r):
            into[r, :] = (into[r, :].astype(jnp.float32) + other[r, :].astype(jnp.float32)).astype(jnp.bfloat16)

        by_rows(into, body)

    sent = []
    waited = set()

    def loaded(p, away):
        if (p, away % n) not in waited:
            waited.add((p, away % n))
            loads[p, away % n].wait()

    for h in range(plan.far, 0, -1):
        order = [plan.order(s, h) for s in (0, 1)]
        for i in range(max(map(len, order))):
            for s in (0, 1):
                if i >= len(order[s]):
                    continue
                p = order[s][i]
                loaded(p, signed(s, h))
                if plan.hops[p][s] > h:
                    reduce_copy(p, s, h + 1).wait_recv()
                    add(term(p, signed(s, h)), slot(p, s, h + 1))
                copy = reduce_copy(p, s, h)
                copy.start()
                sent.append(copy)

    def gather_copy(p, side, hop, back):
        k, layer, _, _ = where[p]
        block = w_out[k].at[layer, rows(p, at(-signed(side, hop - back)))]
        return pltpu.make_async_remote_copy(
            src_ref=block,
            dst_ref=block,
            send_sem=gather_send_sem.at[p, side, hop - 1],
            recv_sem=gather_recv_sem.at[p, side, hop - 1],
            device_id={"dp": to[side]},
            device_id_type=MESH,
        )

    def step(p):
        k, layer, kind, place = where[p]
        first_row = me * m[k].shape[1]

        def body(r):
            total = term(p, 0)[r, :].astype(jnp.float32)
            for s in (0, 1):
                total += slot(p, s, 1)[r, :].astype(jnp.float32)
            total = total.astype(jnp.bfloat16).astype(jnp.float32)
            new = adamw(own[kind].at[place][r, :].astype(jnp.float32), m_in[kind].at[place][r, :], v_in[kind].at[place][r, :], total)
            w_out[k].at[layer][pl.ds(pl.multiple_of(first_row + r.start, ROWS), ROWS), :] = new[0]
            m_out[k].at[layer][r, :] = new[1]
            v_out[k].at[layer][r, :] = new[2]

        by_rows(term(p, 0), body)

    for p in range(pieces):
        k, layer, _, _ = where[p]
        if layer == 0:
            for copy in states[k]:
                copy.wait()
        loaded(p, 0)
        for s in (0, 1):
            reduce_copy(p, s, 1).wait_recv()
        step(p)
        for s in (0, 1):
            copy = gather_copy(p, s, 1, 1)
            copy.start()
            sent.append(copy)

    for hop in range(2, plan.far + 1):
        order = [plan.spread(s, hop) for s in (0, 1)]
        for i in range(max(map(len, order))):
            for s in (0, 1):
                if i < len(order[s]):
                    p = order[s][i]
                    gather_copy(p, s, hop - 1, 0).wait_recv()
                    copy = gather_copy(p, s, hop, 1)
                    copy.start()
                    sent.append(copy)
    for p in range(pieces):
        for s in (0, 1):
            gather_copy(p, s, plan.hops[p][s], 0).wait_recv()
    for copy in sent:
        copy.wait_send()


def solution(mesh):
    n = mesh.shape["dp"]

    def step(*arrays):
        g, w, m, v = (arrays[i : i + 3] for i in (0, 3, 6, 9))
        layers = w[0].shape[0]
        plan = Plan(n, layers * len(w))
        kinds, names = [], []
        for one in m:
            if one.shape[1:] not in kinds:
                kinds.append(one.shape[1:])
            kind = kinds.index(one.shape[1:])
            names.append((kind, sum(1 for other, _ in names if other == kind)))
        count = [layers * sum(1 for kind, _ in names if kind == i) for i in range(len(kinds))]
        places = list(zip(count, kinds, strict=True))
        hbm, vmem = pl.BlockSpec(memory_space=pltpu.HBM), pl.BlockSpec(memory_space=pltpu.VMEM)
        pieces, far = plan.pieces, plan.far
        dma = pltpu.SemaphoreType.DMA
        out = pl.pallas_call(
            functools.partial(kernel, plan, kinds, names),
            out_shape=[pltpu.VMEM(one.shape, one.dtype) for one in (*w, *m, *v)],
            in_specs=[hbm] * len(arrays),
            out_specs=[vmem] * 9,
            scratch_shapes=[
                *(pltpu.VMEM((c, n, *shape), jnp.bfloat16) for c, shape in places),
                *(pltpu.VMEM((c, 2 * far, *shape), jnp.bfloat16) for c, shape in places),
                *(pltpu.VMEM((c, *shape), jnp.bfloat16) for c, shape in places),
                *(pltpu.VMEM((c, *shape), jnp.float32) for c, shape in places),
                *(pltpu.VMEM((c, *shape), jnp.float32) for c, shape in places),
                dma((pieces, n)),
                dma((len(w), 3)),
                dma((pieces, 2, far)),
                dma((pieces, 2, far)),
                dma((pieces, 2, far)),
                dma((pieces, 2, far)),
            ],
            compiler_params=pltpu.CompilerParams(collective_id=0, has_side_effects=True, vmem_limit_bytes=VMEM),
        )(*arrays)
        return tuple(out)

    all_of, cut = P(None, None, None), P(None, "dp", None)
    return jax.shard_map(
        step,
        mesh=mesh,
        in_specs=(P(("rep", "dp"), None, None, None),) * 3 + (all_of,) * 3 + (cut,) * 6,
        out_specs=(P("rep", None, None),) * 3 + (P("rep", "dp", None),) * 6,
        check_vma=False,
    )
```

time: 282 us -> 184 us (0.65)
  waiting for transfers between devices: 252 us -> 0 us
  Pallas kernels: 0 us -> 174 us
  between operations: 14.2 us -> 0.66 us
  other arithmetic: 7.47 us -> 0 us
    pallas_call x0 -> x1, Pallas kernels: none -> 174 us  [step(): pl.pallas_call(functools.partial(kernel, plan, kinds, names), out_shape=[...]
    reduce_scatter x3 -> x0, waiting for transfers between devices: 129 us -> none  [step(): lax.psum_scatter(t[0], 'dp', scatter_dimension=1, tiled=True)]
    all_gather x3 -> x0, waiting for transfers between devices: 120 us -> none  [step(): whole = [lax.all_gather(one[0], 'dp', axis=1, tiled=True) for one in new]]
    convert_element_type x3 -> x0, other arithmetic: 7.47 us -> none  [adamw(): return ((w - 0.02 * step).astype(jnp.bfloat16), m, v)]
    unnamed x19 -> x9, local copies, waits for them, and re-layouts: 8.22 us -> 9.88 us
  transfers between devices with their start and end apart: 6 -> 0, of which waited for: 6 -> 0; matrix products, arithmetic and copies ran while one was open for 3% -> 0% of each run, Pallas kernels for 0% -> 0%
where the time goes in v1:
time: 184 us
  Pallas kernels  174 us (95%)
  local copies, waits for them, and re-layouts  9.88 us (5%)
    pallas_call x1, Pallas kernels, step(): pl.pallas_call(functools.partial(kernel, plan, kinds, names), out_shape=[...  174 us
    unnamed x9, local copies, waits for them, and re-layouts  9.88 us

profile of v1, /device:TPU:22, one launch (start us, length us, event | category | flops | bytes accessed | tf_op | source)
XLA Modules:
  0.0 184.1 jit_solution(16118145006020194156)
XLA Ops:
  0.6 173.6 %shard_map.187 = (bf16[2,512,1408]{2,1,0:T(8,128)(2,1)S(1)}, bf16[2,512,1408]{2,1,0:T(8,128)(2,1)S(1)}, bf16[2,1408,512]{2,1,0:T(8,128)(2,1)S(1)}, f32[2,64,1408...) custom-call(bf16[1,2,512,1408]{3,2,1,0:T(8,128)(2,1)} %refs_0_.1, ...), custom_call_target="tpu_custom_call" | custom-call | tf_op jit(solution)/shard_map/pallas_call | solution.py:230
  174.2 1.6 copy.30
  175.8 0.9 copy.33
  176.7 0.9 copy.34
  177.5 0.9 copy.35
  178.4 0.9 copy.36
  179.2 0.9 copy.37
  180.1 0.9 copy.38
  181.0 1.6 copy.31
  182.5 1.6 copy.32

commit v2 on v1

--- a/solution.py
+++ b/solution.py
@@ -26,11 +26,11 @@
         self.hops = [(far, near) if p % 2 == 0 else (near, far) for p in range(pieces)]
         self.far = far
 
+    def starts(self, side, hops_left):
+        return [p for p in range(self.pieces) if self.hops[p][side] == hops_left]
+
     def order(self, side, hops_left):
-        live = [p for p in range(self.pieces) if self.hops[p][side] >= hops_left]
-        if hops_left == self.far - 1:
-            live.sort(key=lambda p: self.hops[p][side])
-        return live
+        return [p for p in range(self.pieces) if self.hops[p][side] > hops_left]
 
     def spread(self, side, hop):
         live = [p for p in range(self.pieces) if self.hops[p][side] >= hop]
@@ -88,29 +88,17 @@
             pltpu.make_async_copy(v[k], v_in[kind].at[mine], state_sem.at[k, 2]),
         ]
 
-    loads = {}
-    first_wave = [(p, s, plan.hops[p][s]) for h in (plan.far, plan.far - 1) for p in range(pieces) for s in (0, 1) if plan.hops[p][s] == h]
-    wanted = [(p, signed(s, h)) for p, s, h in first_wave]
-    for h in range(plan.far - 1, 0, -1):
-        wanted += [(p, signed(s, h)) for p in range(pieces) for s in (0, 1)]
-    wanted += [(p, 0) for p in range(pieces)]
-    for p, away in wanted:
-        if (p, away % n) not in loads:
-            loads[p, away % n] = load(p, away)
-            loads[p, away % n].start()
-    states = [state_loads(k) for k in range(weights)]
-    for copies in states:
-        for copy in copies:
-            copy.start()
-
     barrier = pltpu.get_barrier_semaphore()
     for neighbour in to:
         pl.semaphore_signal(barrier, inc=1, device_id={"dp": neighbour}, device_id_type=MESH)
     pl.semaphore_wait(barrier, 2)
 
     def reduce_copy(p, side, hops_left):
+        k, layer, _, _ = where[p]
+        away = signed(side, hops_left)
+        first = plan.hops[p][side] == hops_left
         return pltpu.make_async_remote_copy(
-            src_ref=term(p, signed(side, hops_left)),
+            src_ref=g[k].at[0, layer, rows(p, at(away))] if first else term(p, away),
             dst_ref=slot(p, side, hops_left),
             send_sem=send_sem.at[p, side, hops_left - 1],
             recv_sem=recv_sem.at[p, side, hops_left - 1],
@@ -127,28 +115,32 @@
 
         by_rows(into, body)
 
-    sent = []
-    waited = set()
-
-    def loaded(p, away):
-        if (p, away % n) not in waited:
-            waited.add((p, away % n))
-            loads[p, away % n].wait()
-
+    sent, loads = [], {}
     for h in range(plan.far, 0, -1):
-        order = [plan.order(s, h) for s in (0, 1)]
-        for i in range(max(map(len, order))):
-            for s in (0, 1):
-                if i >= len(order[s]):
-                    continue
-                p = order[s][i]
-                loaded(p, signed(s, h))
-                if plan.hops[p][s] > h:
-                    reduce_copy(p, s, h + 1).wait_recv()
-                    add(term(p, signed(s, h)), slot(p, s, h + 1))
-                copy = reduce_copy(p, s, h)
-                copy.start()
-                sent.append(copy)
+        for order in zip(*(plan.starts(s, h) for s in (0, 1)), strict=True):
+            for s, p in enumerate(order):
+                sent.append(reduce_copy(p, s, h))
+                sent[-1].start()
+    for h in range(plan.far - 1, -1, -1):
+        for p in range(pieces):
+            for away in sorted({h, -h}):
+                if h == 0 or plan.hops[p][away < 0] > h:
+                    loads[p, away] = load(p, away)
+                    loads[p, away].start()
+    states = [state_loads(k) for k in range(weights)]
+    for copies in states:
+        for copy in copies:
+            copy.start()
+
+    for h in range(plan.far - 1, 0, -1):
+        for order in zip(*(plan.order(s, h) for s in (0, 1)), strict=True):
+            for s, p in enumerate(order):
+                away = signed(s, h)
+                loads[p, away].wait()
+                reduce_copy(p, s, h + 1).wait_recv()
+                add(term(p, away), slot(p, s, h + 1))
+                sent.append(reduce_copy(p, s, h))
+                sent[-1].start()
 
     def gather_copy(p, side, hop, back):
         k, layer, _, _ = where[p]
@@ -183,7 +175,7 @@
         if layer == 0:
             for copy in states[k]:
                 copy.wait()
-        loaded(p, 0)
+        loads[p, 0].wait()
         for s in (0, 1):
             reduce_copy(p, s, 1).wait_recv()
         step(p)
@@ -207,6 +199,26 @@
             gather_copy(p, s, plan.hops[p][s], 0).wait_recv()
     for copy in sent:
         copy.wait_send()
+
+
+def put_kernel(count, *refs):
+    sources, results, sem = refs[:count], refs[count:-1], refs[-1]
+    copies = [pltpu.make_async_copy(a, b, sem.at[i]) for i, (a, b) in enumerate(zip(sources, results, strict=True))]
+    for copy in copies:
+        copy.start()
+    for copy in copies:
+        copy.wait()
+
+
+def put(arrays):
+    return pl.pallas_call(
+        functools.partial(put_kernel, len(arrays)),
+        out_shape=[pltpu.HBM(one.shape, one.dtype) for one in arrays],
+        in_specs=[pl.BlockSpec(memory_space=pltpu.VMEM)] * len(arrays),
+        out_specs=[pl.BlockSpec(memory_space=pltpu.HBM)] * len(arrays),
+        scratch_shapes=[pltpu.SemaphoreType.DMA((len(arrays),))],
+        compiler_params=pltpu.CompilerParams(vmem_limit_bytes=1 << 20),
+    )(*arrays)
 
 
 def solution(mesh):
@@ -247,7 +259,7 @@
             ],
             compiler_params=pltpu.CompilerParams(collective_id=0, has_side_effects=True, vmem_limit_bytes=VMEM),
         )(*arrays)
-        return tuple(out)
+        return tuple(put(out))
 
     all_of, cut = P(None, None, None), P(None, "dp", None)
     return jax.shard_map(

time: 184 us -> 179 us (0.973)
  local copies, waits for them, and re-layouts: 9.88 us -> 0 us
  Pallas kernels: 174 us -> 178 us
    unnamed x9 -> x0, local copies, waits for them, and re-layouts: 9.88 us -> none
    pallas_call x0 -> x1, Pallas kernels: none -> 4.79 us  [put(): pl.pallas_call(functools.partial(put_kernel, len(arrays)), out_shape=[plt...]
where the time goes in v2:
time: 179 us
  Pallas kernels  178 us (99%)
    pallas_call x1, Pallas kernels, step(): pl.pallas_call(functools.partial(kernel, plan, kinds, names), out_shape=[...  173 us
    pallas_call x1, Pallas kernels, put(): pl.pallas_call(functools.partial(put_kernel, len(arrays)), out_shape=[plt...  4.79 us

profile of v2, /device:TPU:22, one launch (start us, length us, event | category | flops | bytes accessed | tf_op | source)
XLA Modules:
  0.0 178.6 jit_solution(6049183936460778562)
XLA Ops:
  0.6 173.2 %shard_map.187 = (bf16[2,512,1408]{2,1,0:T(8,128)(2,1)S(1)}, bf16[2,512,1408]{2,1,0:T(8,128)(2,1)S(1)}, bf16[2,1408,512]{2,1,0:T(8,128)(2,1)S(1)}, f32[2,64,1408...) custom-call(bf16[1,2,512,1408]{3,2,1,0:T(8,128)(2,1)} %refs_0_.1, ...), custom_call_target="tpu_custom_call" | custom-call | tf_op jit(solution)/shard_map/pallas_call | solution.py:242
  173.8 4.8 %shard_map.188 = (bf16[2,512,1408]{2,1,0:T(8,128)(2,1)}, bf16[2,512,1408]{2,1,0:T(8,128)(2,1)}, bf16[2,1408,512]{2,1,0:T(8,128)(2,1)}, f32[2,64,1408]{2,1,0:T(8,...) custom-call(bf16[2,512,1408]{2,1,0:T(8,128)(2,1)S(1)} %get-tuple-ele, ...), custom_call_target="tpu_custom_call" | custom-call | tf_op jit(solution)/shard_map/pallas_call | solution.py:214

commit v3 on v0

v3 whole, which is shorter than its diff:
```python
import functools

import jax
import jax.numpy as jnp
from jax import lax
from jax.experimental import pallas as pl
from jax.experimental.pallas import tpu as pltpu
from jax.sharding import PartitionSpec as P

MESH = pl.DeviceIdType.MESH
DMA = pltpu.SemaphoreType.DMA
HBM, VMEM = pl.BlockSpec(memory_space=pltpu.HBM), pl.BlockSpec(memory_space=pltpu.VMEM)
ROWS = 16
GRANT_EARLY, GRANT_LATE = 57_000_000, 61_500_000


def adamw(w, m, v, g):
    m = 0.9 * m + 0.1 * g
    v = 0.95 * v + 0.05 * g * g
    step = m * lax.rsqrt(v + 1e-8) + 0.1 * w
    return (w - 0.02 * step).astype(jnp.bfloat16), m, v


def by_rows(count, body):
    lax.fori_loop(0, count // ROWS, lambda i, _: body(pl.multiple_of(i * ROWS, ROWS)), None)


def side_of(away):
    return 0 if away > 0 else 1


class Ring:
    def __init__(self, n, me, g, w, m, v, results, buffers, sems):
        self.n, self.me, self.g, self.w, self.m, self.v = n, me, g, w, m, v
        self.w_out, self.m_out, self.v_out = results
        self.terms, self.inbox, self.total, self.own, self.m_in, self.v_in = buffers
        self.load_sem, self.state_sem, self.send_sem, self.recv_sem, self.gather_send_sem, self.gather_recv_sem = sems
        self.to = [lax.rem(me + 1, n), lax.rem(me + n - 1, n)]
        self.layers = g[0].shape[1]
        self.pieces = len(g) * self.layers
        self.rows = g[0].shape[2] // n
        self.far = n // 2
        near = (n - 1) // 2
        self.hops = [(self.far, near) if p % 2 == 0 else (near, self.far) for p in range(self.pieces)]

    @staticmethod
    def buffers(n, pieces, shape, state):
        far = n // 2
        data = [pltpu.VMEM((pieces, n, *shape), jnp.bfloat16), pltpu.VMEM((pieces, 2, far, *shape), jnp.bfloat16)]
        if state:
            data += [pltpu.VMEM((pieces, *shape), t) for t in (jnp.bfloat16, jnp.bfloat16, jnp.float32, jnp.float32)]
        return data

    @staticmethod
    def sems(n, pieces, weights):
        far = n // 2
        return [DMA((pieces, n)), DMA((weights, 3)), *(DMA((pieces, 2, far)) for _ in range(4))]

    def at(self, away):
        return lax.rem(self.me + (away + self.n), self.n)

    def block(self, owner):
        return pl.ds(pl.multiple_of(owner * self.rows, self.rows), self.rows)

    def mine(self, p, away):
        return self.g[p // self.layers].at[0, p % self.layers, self.block(self.at(away))]

    def load(self, p, away):
        return pltpu.make_async_copy(self.mine(p, away), self.terms.at[p, away % self.n], self.load_sem.at[p, away % self.n])

    def remote(self, side, source, target, send_sem, recv_sem):
        return pltpu.make_async_remote_copy(
            src_ref=source, dst_ref=target, send_sem=send_sem, recv_sem=recv_sem, device_id={"dp": self.to[side]}, device_id_type=MESH
        )

    def sum_copy(self, p, side, left):
        away = left if side == 0 else -left
        source = self.mine(p, away) if self.hops[p][side] == left else self.terms.at[p, away % self.n]
        at = (p, side, left - 1)
        return self.remote(side, source, self.inbox.at[at], self.send_sem.at[at], self.recv_sem.at[at])

    def gather_copy(self, p, side, hop, back):
        away = hop - back
        block = self.w_out[p // self.layers].at[p % self.layers, self.block(self.at(-away if side == 0 else away))]
        at = (p, side, hop - 1)
        return self.remote(side, block, block, self.gather_send_sem.at[at], self.gather_recv_sem.at[at])

    def live(self, side, hops):
        return [p for p in range(self.pieces) if self.hops[p][side] >= hops]

    def first_terms(self):
        for left in range(self.far, 0, -1):
            for order in zip(*([p for p in range(self.pieces) if self.hops[p][s] == left] for s in (0, 1)), strict=True):
                for s, p in enumerate(order):
                    self.sum_copy(p, s, left).start()

    def loaded(self):
        return [
            (p, away)
            for left in range(self.far - 1, -1, -1)
            for p in range(self.pieces)
            for away in sorted({left, -left})
            if left == 0 or self.hops[p][side_of(away)] > left
        ]

    def load_terms(self):
        for p, away in self.loaded():
            self.load(p, away).start()

    def states(self, k):
        mine, block = pl.ds(k * self.layers, self.layers), self.block(self.me)
        return [
            pltpu.make_async_copy(self.w[k].at[:, block], self.own.at[mine], self.state_sem.at[k, 0]),
            pltpu.make_async_copy(self.m[k], self.m_in.at[mine], self.state_sem.at[k, 1]),
            pltpu.make_async_copy(self.v[k], self.v_in.at[mine], self.state_sem.at[k, 2]),
        ]

    def load_states(self):
        for k in range(len(self.g)):
            for copy in self.states(k):
                copy.start()

    def pass_on(self):
        for left in range(self.far - 1, 0, -1):
            for order in zip(*(self.live(s, left + 1) for s in (0, 1)), strict=True):
                for s, p in enumerate(order):
                    away = left if s == 0 else -left
                    self.load(p, away).wait()
                    self.sum_copy(p, s, left + 1).wait_recv()
                    here, came = self.terms.at[p, away % self.n], self.inbox.at[p, s, left]

                    def add(r, here=here, came=came):
                        r = pl.ds(r, ROWS)
                        here[r, :] = (here[r, :].astype(jnp.float32) + came[r, :].astype(jnp.float32)).astype(jnp.bfloat16)

                    by_rows(self.rows, add)
                    self.sum_copy(p, s, left).start()

    def finish_sum(self, p):
        self.load(p, 0).wait()
        for s in (0, 1):
            self.sum_copy(p, s, 1).wait_recv()

        def add(r):
            r = pl.ds(r, ROWS)
            parts = [ref[r, :].astype(jnp.float32) for ref in (self.terms.at[p, 0], self.inbox.at[p, 0, 0], self.inbox.at[p, 1, 0])]
            self.total.at[p][r, :] = (parts[0] + parts[1] + parts[2]).astype(jnp.bfloat16)

        by_rows(self.rows, add)

    def sums_sent(self):
        for p in range(self.pieces):
            for s in (0, 1):
                for left in range(1, self.hops[p][s] + 1):
                    self.sum_copy(p, s, left).wait_send()

    def step(self, p):
        k, layer = p // self.layers, p % self.layers
        if layer == 0:
            for copy in self.states(k):
                copy.wait()

        def take(r):
            rows = pl.ds(r, ROWS)
            w, m, v, g = (ref.at[p][rows, :] for ref in (self.own, self.m_in, self.v_in, self.total))
            new = adamw(w.astype(jnp.float32), m, v, g.astype(jnp.float32))
            self.w_out[k].at[layer][pl.ds(pl.multiple_of(self.me * self.rows + r, ROWS), ROWS), :] = new[0]
            self.m_out[k].at[layer][rows, :] = new[1]
            self.v_out[k].at[layer][rows, :] = new[2]

        by_rows(self.rows, take)
        for s in (0, 1):
            self.gather_copy(p, s, 1, 1).start()

    def gather(self):
        for hop in range(2, self.far + 1):
            order = [self.live(s, hop) for s in (0, 1)]
            for s in (0, 1):
                if hop == self.far - 1:
                    order[s].sort(key=lambda p, s=s: -self.hops[p][s])
            for pair in zip(*order, strict=True):
                for s, p in enumerate(pair):
                    self.gather_copy(p, s, hop - 1, 0).wait_recv()
                    self.gather_copy(p, s, hop, 1).start()
        for p in range(self.pieces):
            for s in (0, 1):
                self.gather_copy(p, s, self.hops[p][s], 0).wait_recv()
                for hop in range(1, self.hops[p][s] + 1):
                    self.gather_copy(p, s, hop, 1).wait_send()

    def greet(self):
        barrier = pltpu.get_barrier_semaphore()
        for neighbour in self.to:
            pl.semaphore_signal(barrier, inc=1, device_id={"dp": neighbour}, device_id_type=MESH)
        pl.semaphore_wait(barrier, 2)


def odd():
    return lax.rem(lax.axis_index("rep"), 2) == 1


def even():
    return lax.rem(lax.axis_index("rep"), 2) == 0


def early_kernel(n, count, *refs):
    refs = list(refs)
    take = lambda c: [refs.pop(0) for _ in range(c)]
    e, l = count
    g, w, m, v, late_g = take(e), take(e), take(e), take(e), take(l)
    results, late_total = [take(e) for _ in range(3)], refs.pop(0)
    me = lax.axis_index("dp")
    ring = Ring(n, me, g, w, m, v, results, take(6), take(6))
    terms, inbox = take(2)
    late = Ring(n, me, late_g, None, None, None, (None,) * 3, (terms, inbox, late_total, None, None, None), take(6))

    ring.greet()

    @pl.when(odd())
    def _():
        late.first_terms()

    ring.first_terms()

    @pl.when(odd())
    def _():
        late.load_terms()

    ring.load_terms()
    ring.load_states()

    @pl.when(odd())
    def _():
        late.pass_on()
        for p in range(late.pieces):
            late.finish_sum(p)
        late.sums_sent()

    ring.pass_on()
    for p in range(ring.pieces):
        ring.finish_sum(p)
        ring.step(p)
    ring.gather()
    ring.sums_sent()


def late_kernel(n, count, *refs):
    refs = list(refs)
    take = lambda c: [refs.pop(0) for _ in range(c)]
    g, w, m, v, total = take(count), take(count), take(count), take(count), refs.pop(0)
    results = [take(count) for _ in range(3)]
    ring = Ring(n, lax.axis_index("dp"), g, w, m, v, results, take(6), take(6))
    total_sem = refs.pop(0)
    ring.greet()

    @pl.when(even())
    def _():
        ring.first_terms()
        ring.load_terms()

    ring.load_states()

    @pl.when(odd())
    def _():
        copy = pltpu.make_async_copy(total, ring.total, total_sem)
        copy.start()
        copy.wait()

    @pl.when(even())
    def _():
        ring.pass_on()
        for p in range(ring.pieces):
            ring.finish_sum(p)
        ring.sums_sent()

    for p in range(ring.pieces):
        ring.step(p)
    ring.gather()


def put_kernel(count, *refs):
    sources, results, sem = refs[:count], refs[count:-1], refs[-1]
    copies = [pltpu.make_async_copy(a, b, sem.at[i]) for i, (a, b) in enumerate(zip(sources, results, strict=True))]
    for copy in copies:
        copy.start()
    for copy in copies:
        copy.wait()


def put(arrays):
    count = len(arrays)
    return pl.pallas_call(
        functools.partial(put_kernel, count),
        out_shape=[pltpu.HBM(one.shape, one.dtype) for one in arrays],
        in_specs=[VMEM] * count,
        out_specs=[HBM] * count,
        scratch_shapes=[DMA((count,))],
        compiler_params=pltpu.CompilerParams(vmem_limit_bytes=1 << 20),
    )(*arrays)


def solution(mesh):
    n = mesh.shape["dp"]

    def step(*arrays):
        g, w, m, v = (arrays[i : i + 3] for i in (0, 3, 6, 9))
        early, late = slice(0, 2), slice(2, 3)
        e, l = len(g[early]), len(g[late])
        layers = w[0].shape[0]
        vmem = lambda several: [pltpu.VMEM(one.shape, one.dtype) for one in several]
        early_shape, late_shape = m[early][0].shape[1:], m[late][0].shape[1:]

        *first, total = pl.pallas_call(
            functools.partial(early_kernel, n, (e, l)),
            out_shape=[*vmem((*w[early], *m[early], *v[early])), pltpu.VMEM((l * layers, *late_shape), jnp.bfloat16)],
            in_specs=[HBM] * (4 * e + l),
            out_specs=[VMEM] * (3 * e + 1),
            scratch_shapes=[
                *Ring.buffers(n, e * layers, early_shape, True),
                *Ring.sems(n, e * layers, e),
                *Ring.buffers(n, l * layers, late_shape, False),
                *Ring.sems(n, l * layers, l),
            ],
            compiler_params=pltpu.CompilerParams(collective_id=0, has_side_effects=True, vmem_limit_bytes=GRANT_EARLY),
        )(*g[early], *w[early], *m[early], *v[early], *g[late])
        *first, total = put([*first, total])
        second = pl.pallas_call(
            functools.partial(late_kernel, n, l),
            out_shape=vmem((*w[late], *m[late], *v[late])),
            in_specs=[HBM] * (4 * l + 1),
            out_specs=[VMEM] * (3 * l),
            scratch_shapes=[*Ring.buffers(n, l * layers, late_shape, True), *Ring.sems(n, l * layers, l), DMA],
            compiler_params=pltpu.CompilerParams(collective_id=1, has_side_effects=True, vmem_limit_bytes=GRANT_LATE),
        )(*g[late], *w[late], *m[late], *v[late], total)
        second = put(second)
        return tuple(one for i in range(3) for one in (*first[i * e : (i + 1) * e], *second[i * l : (i + 1) * l]))

    all_of, cut = P(None, None, None), P(None, "dp", None)
    return jax.shard_map(
        step,
        mesh=mesh,
        in_specs=(P(("rep", "dp"), None, None, None),) * 3 + (all_of,) * 3 + (cut,) * 6,
        out_specs=(P("rep", None, None),) * 3 + (P("rep", "dp", None),) * 6,
        check_vma=False,
    )
```

time: 282 us -> 178 us (0.63)
  waiting for transfers between devices: 252 us -> 0 us
  Pallas kernels: 0 us -> 177 us
  between operations: 14.2 us -> 0.67 us
  local copies, waits for them, and re-layouts: 8.22 us -> 0 us
  other arithmetic: 7.47 us -> 0 us
    pallas_call x0 -> x4, Pallas kernels: none -> 177 us  [the longest x1 115 us: step(): pl.pallas_call(functools.partial(early_kernel, n, (e, l)), out_shape=[*vm...]
    reduce_scatter x3 -> x0, waiting for transfers between devices: 129 us -> none  [step(): lax.psum_scatter(t[0], 'dp', scatter_dimension=1, tiled=True)]
    all_gather x3 -> x0, waiting for transfers between devices: 120 us -> none  [step(): whole = [lax.all_gather(one[0], 'dp', axis=1, tiled=True) for one in new]]
    unnamed x19 -> x0, local copies, waits for them, and re-layouts: 8.22 us -> none
    convert_element_type x3 -> x0, other arithmetic: 7.47 us -> none  [adamw(): return ((w - 0.02 * step).astype(jnp.bfloat16), m, v)]
  transfers between devices with their start and end apart: 6 -> 0, of which waited for: 6 -> 0; matrix products, arithmetic and copies ran while one was open for 3% -> 0% of each run, Pallas kernels for 0% -> 0%
where the time goes in v3:
time: 178 us
  Pallas kernels  177 us (99%)
    pallas_call x1, Pallas kernels, step(): pl.pallas_call(functools.partial(early_kernel, n, (e, l)), out_shape=[*vm...  115 us
    pallas_call x1, Pallas kernels, step(): pl.pallas_call(functools.partial(late_kernel, n, l), out_shape=vmem((*w[l...  57.2 us
    pallas_call x2, Pallas kernels, put(): pl.pallas_call(functools.partial(put_kernel, count), out_shape=[pltpu.HBM...  5.64 us

profile of v3, /device:TPU:22, one launch (start us, length us, event | category | flops | bytes accessed | tf_op | source)
XLA Modules:
  0.0 178.0 jit_solution(6437818320238677960)
XLA Ops:
  0.6 114.5 %shard_map.187 = (bf16[2,512,1408]{2,1,0:T(8,128)(2,1)S(1)}, bf16[2,512,1408]{2,1,0:T(8,128)(2,1)S(1)}, f32[2,64,1408]{2,1,0:T(8,128)S(1)}, f32[2,64,1408]{2,1,0...) custom-call(bf16[1,2,512,1408]{3,2,1,0:T(8,128)(2,1)} %refs_0_.2, ...), custom_call_target="tpu_custom_call" | custom-call | tf_op jit(solution)/shard_map/pallas_call | solution.py:313
  115.2 3.6 %shard_map.188 = (bf16[2,512,1408]{2,1,0:T(8,128)(2,1)}, bf16[2,512,1408]{2,1,0:T(8,128)(2,1)}, f32[2,64,1408]{2,1,0:T(8,128)}, f32[2,64,1408]{2,1,0:T(8,128)}, ...) custom-call(bf16[2,512,1408]{2,1,0:T(8,128)(2,1)S(1)} %get-tuple-element.29.refs_0_, ...), custom_call_target="tpu_custom_call" | custom-call | tf_op jit(solution)/shard_map/pallas_call | solution.py:292
  118.8 57.2 %shard_map.189 = (bf16[2,1408,512]{2,1,0:T(8,128)(2,1)S(1)}, f32[2,176,512]{2,1,0:T(8,128)S(1)}, f32[2,176,512]{2,1,0:T(8,128)S(1)}) custom-call(bf16[1,2,1408,512]{3,2,1,0:T(8,128)(2,1)} %refs_0_.3, bf16[2,1408,512]{2,1,0:T(8,128)(2,1)} %refs_1_.3, f32[2,176,512]{2,1,0:T(8,128)} %refs_2_.3, f32[2,176,512]{2,1,0:T(8,128)} %refs_3_.3, ...), custom_call_target="tpu_custom_call" | custom-call | tf_op jit(solution)/shard_map/pallas_call | solution.py:327
  176.0 2.1 %shard_map.190 = (bf16[2,1408,512]{2,1,0:T(8,128)(2,1)}, f32[2,176,512]{2,1,0:T(8,128)}, f32[2,176,512]{2,1,0:T(8,128)}) custom-call(bf16[2,1408,512]{2,1,0:T(8,128)(2,1)S(1)} %get-tuple-element.39.refs_0_, f32[2,176,512]{2,1,0:T(8,128)S(1)} %get-tuple-element.40.refs_1_, f32[2,176,512]{2,1,0:T(8,128)S(1)} %get-tuple-element.41.refs_2_), custom_call_target="tpu_custom_call" | custom-call | tf_op jit(solution)/shard_map/pallas_call | solution.py:292

commit v4 on v3

--- a/solution.py
+++ b/solution.py
@@ -11,6 +11,7 @@
 DMA = pltpu.SemaphoreType.DMA
 HBM, VMEM = pl.BlockSpec(memory_space=pltpu.HBM), pl.BlockSpec(memory_space=pltpu.VMEM)
 ROWS = 16
+EARLY_PIECES, LATE_PIECES = 2, 4
 GRANT_EARLY, GRANT_LATE = 57_000_000, 61_500_000
 
 
@@ -30,43 +31,65 @@
 
 
 class Ring:
-    def __init__(self, n, me, g, w, m, v, results, buffers, sems):
+    def __init__(self, n, me, pieces, g, w, m, v, results, buffers, sems):
         self.n, self.me, self.g, self.w, self.m, self.v = n, me, g, w, m, v
         self.w_out, self.m_out, self.v_out = results
         self.terms, self.inbox, self.total, self.own, self.m_in, self.v_in = buffers
         self.load_sem, self.state_sem, self.send_sem, self.recv_sem, self.gather_send_sem, self.gather_recv_sem = sems
         self.to = [lax.rem(me + 1, n), lax.rem(me + n - 1, n)]
         self.layers = g[0].shape[1]
-        self.pieces = len(g) * self.layers
-        self.rows = g[0].shape[2] // n
+        self.block_rows = g[0].shape[2] // n
+        self.parts = self.cut(len(g), self.layers, self.block_rows, pieces)
+        self.pieces = len(self.parts)
         self.far = n // 2
         near = (n - 1) // 2
-        self.hops = [(self.far, near) if p % 2 == 0 else (near, self.far) for p in range(self.pieces)]
+        self.hops = [(self.far, near) if turn == 0 else (near, self.far) for *_, turn in self.parts]
 
     @staticmethod
-    def buffers(n, pieces, shape, state):
+    def cut(weights, layers, rows, pieces):
+        size = -(-rows // (pieces * ROWS)) * ROWS
+        starts = range(0, rows, size)
+        return [(k, layer, r, min(size, rows - r), (i + layer) % 2) for k in range(weights) for layer in range(layers) for i, r in enumerate(starts)]
+
+    @classmethod
+    def buffers(cls, n, pieces, weights, layers, shape, state):
         far = n // 2
+        parts = cls.cut(weights, layers, shape[0], pieces)
+        pieces, whole = len(parts), (weights * layers, *shape)
+        shape = (parts[0][3], shape[1])
         data = [pltpu.VMEM((pieces, n, *shape), jnp.bfloat16), pltpu.VMEM((pieces, 2, far, *shape), jnp.bfloat16)]
         if state:
-            data += [pltpu.VMEM((pieces, *shape), t) for t in (jnp.bfloat16, jnp.bfloat16, jnp.float32, jnp.float32)]
+            data += [pltpu.VMEM(whole, t) for t in (jnp.bfloat16, jnp.bfloat16, jnp.float32, jnp.float32)]
         return data
 
-    @staticmethod
-    def sems(n, pieces, weights):
+    @classmethod
+    def sems(cls, n, pieces, weights, layers, shape):
         far = n // 2
+        pieces = len(cls.cut(weights, layers, shape[0], pieces))
         return [DMA((pieces, n)), DMA((weights, 3)), *(DMA((pieces, 2, far)) for _ in range(4))]
 
     def at(self, away):
         return lax.rem(self.me + (away + self.n), self.n)
 
     def block(self, owner):
-        return pl.ds(pl.multiple_of(owner * self.rows, self.rows), self.rows)
+        return pl.ds(pl.multiple_of(owner * self.block_rows, self.block_rows), self.block_rows)
+
+    def rows(self, p, owner):
+        _, _, first, count, _ = self.parts[p]
+        return pl.ds(pl.multiple_of(owner * self.block_rows + first, ROWS), count)
+
+    def term(self, p, away):
+        return self.terms.at[p, away % self.n, pl.ds(0, self.parts[p][3])]
+
+    def came(self, p, side, left):
+        return self.inbox.at[p, side, left - 1, pl.ds(0, self.parts[p][3])]
 
     def mine(self, p, away):
-        return self.g[p // self.layers].at[0, p % self.layers, self.block(self.at(away))]
+        k, layer, *_ = self.parts[p]
+        return self.g[k].at[0, layer, self.rows(p, self.at(away))]
 
     def load(self, p, away):
-        return pltpu.make_async_copy(self.mine(p, away), self.terms.at[p, away % self.n], self.load_sem.at[p, away % self.n])
+        return pltpu.make_async_copy(self.mine(p, away), self.term(p, away), self.load_sem.at[p, away % self.n])
 
     def remote(self, side, source, target, send_sem, recv_sem):
         return pltpu.make_async_remote_copy(
@@ -75,13 +98,14 @@
 
     def sum_copy(self, p, side, left):
         away = left if side == 0 else -left
-        source = self.mine(p, away) if self.hops[p][side] == left else self.terms.at[p, away % self.n]
+        source = self.mine(p, away) if self.hops[p][side] == left else self.term(p, away)
         at = (p, side, left - 1)
-        return self.remote(side, source, self.inbox.at[at], self.send_sem.at[at], self.recv_sem.at[at])
+        return self.remote(side, source, self.came(p, side, left), self.send_sem.at[at], self.recv_sem.at[at])
 
     def gather_copy(self, p, side, hop, back):
         away = hop - back
-        block = self.w_out[p // self.layers].at[p % self.layers, self.block(self.at(-away if side == 0 else away))]
+        k, layer, *_ = self.parts[p]
+        block = self.w_out[k].at[layer, self.rows(p, self.at(-away if side == 0 else away))]
         at = (p, side, hop - 1)
         return self.remote(side, block, block, self.gather_send_sem.at[at], self.gather_recv_sem.at[at])
 
@@ -127,13 +151,13 @@
                     away = left if s == 0 else -left
                     self.load(p, away).wait()
                     self.sum_copy(p, s, left + 1).wait_recv()
-                    here, came = self.terms.at[p, away % self.n], self.inbox.at[p, s, left]
+                    here, came = self.term(p, away), self.came(p, s, left + 1)
 
                     def add(r, here=here, came=came):
                         r = pl.ds(r, ROWS)
                         here[r, :] = (here[r, :].astype(jnp.float32) + came[r, :].astype(jnp.float32)).astype(jnp.bfloat16)
 
-                    by_rows(self.rows, add)
+                    by_rows(self.parts[p][3], add)
                     self.sum_copy(p, s, left).start()
 
     def finish_sum(self, p):
@@ -141,12 +165,14 @@
         for s in (0, 1):
             self.sum_copy(p, s, 1).wait_recv()
 
+        k, layer, first, count, _ = self.parts[p]
+
         def add(r):
-            r = pl.ds(r, ROWS)
-            parts = [ref[r, :].astype(jnp.float32) for ref in (self.terms.at[p, 0], self.inbox.at[p, 0, 0], self.inbox.at[p, 1, 0])]
-            self.total.at[p][r, :] = (parts[0] + parts[1] + parts[2]).astype(jnp.bfloat16)
-
-        by_rows(self.rows, add)
+            here = pl.ds(r, ROWS)
+            parts = [ref[here, :].astype(jnp.float32) for ref in (self.term(p, 0), self.came(p, 0, 1), self.came(p, 1, 1))]
+            self.total.at[k * self.layers + layer][pl.ds(first + r, ROWS), :] = (parts[0] + parts[1] + parts[2]).astype(jnp.bfloat16)
+
+        by_rows(count, add)
 
     def sums_sent(self):
         for p in range(self.pieces):
@@ -155,20 +181,20 @@
                     self.sum_copy(p, s, left).wait_send()
 
     def step(self, p):
-        k, layer = p // self.layers, p % self.layers
-        if layer == 0:
+        k, layer, first, count, _ = self.parts[p]
+        if layer == 0 and first == 0:
             for copy in self.states(k):
                 copy.wait()
 
         def take(r):
-            rows = pl.ds(r, ROWS)
-            w, m, v, g = (ref.at[p][rows, :] for ref in (self.own, self.m_in, self.v_in, self.total))
+            rows = pl.ds(first + r, ROWS)
+            w, m, v, g = (ref.at[k * self.layers + layer][rows, :] for ref in (self.own, self.m_in, self.v_in, self.total))
             new = adamw(w.astype(jnp.float32), m, v, g.astype(jnp.float32))
-            self.w_out[k].at[layer][pl.ds(pl.multiple_of(self.me * self.rows + r, ROWS), ROWS), :] = new[0]
+            self.w_out[k].at[layer][pl.ds(pl.multiple_of(self.me * self.block_rows + (first + r), ROWS), ROWS), :] = new[0]
             self.m_out[k].at[layer][rows, :] = new[1]
             self.v_out[k].at[layer][rows, :] = new[2]
 
-        by_rows(self.rows, take)
+        by_rows(count, take)
         for s in (0, 1):
             self.gather_copy(p, s, 1, 1).start()
 
@@ -210,9 +236,9 @@
     g, w, m, v, late_g = take(e), take(e), take(e), take(e), take(l)
     results, late_total = [take(e) for _ in range(3)], refs.pop(0)
     me = lax.axis_index("dp")
-    ring = Ring(n, me, g, w, m, v, results, take(6), take(6))
+    ring = Ring(n, me, EARLY_PIECES, g, w, m, v, results, take(6), take(6))
     terms, inbox = take(2)
-    late = Ring(n, me, late_g, None, None, None, (None,) * 3, (terms, inbox, late_total, None, None, None), take(6))
+    late = Ring(n, me, LATE_PIECES, late_g, None, None, None, (None,) * 3, (terms, inbox, late_total, None, None, None), take(6))
 
     ring.greet()
 
@@ -249,7 +275,7 @@
     take = lambda c: [refs.pop(0) for _ in range(c)]
     g, w, m, v, total = take(count), take(count), take(count), take(count), refs.pop(0)
     results = [take(count) for _ in range(3)]
-    ring = Ring(n, lax.axis_index("dp"), g, w, m, v, results, take(6), take(6))
+    ring = Ring(n, lax.axis_index("dp"), LATE_PIECES, g, w, m, v, results, take(6), take(6))
     total_sem = refs.pop(0)
     ring.greet()
 
@@ -316,10 +342,10 @@
             in_specs=[HBM] * (4 * e + l),
             out_specs=[VMEM] * (3 * e + 1),
             scratch_shapes=[
-                *Ring.buffers(n, e * layers, early_shape, True),
-                *Ring.sems(n, e * layers, e),
-                *Ring.buffers(n, l * layers, late_shape, False),
-                *Ring.sems(n, l * layers, l),
+                *Ring.buffers(n, EARLY_PIECES, e, layers, early_shape, True),
+                *Ring.sems(n, EARLY_PIECES, e, layers, early_shape),
+                *Ring.buffers(n, LATE_PIECES, l, layers, late_shape, False),
+                *Ring.sems(n, LATE_PIECES, l, layers, late_shape),
             ],
             compiler_params=pltpu.CompilerParams(collective_id=0, has_side_effects=True, vmem_limit_bytes=GRANT_EARLY),
         )(*g[early], *w[early], *m[early], *v[early], *g[late])
@@ -329,7 +355,7 @@
             out_shape=vmem((*w[late], *m[late], *v[late])),
             in_specs=[HBM] * (4 * l + 1),
             out_specs=[VMEM] * (3 * l),
-            scratch_shapes=[*Ring.buffers(n, l * layers, late_shape, True), *Ring.sems(n, l * layers, l), DMA],
+            scratch_shapes=[*Ring.buffers(n, LATE_PIECES, l, layers, late_shape, True), *Ring.sems(n, LATE_PIECES, l, layers, late_shape), DMA],
             compiler_params=pltpu.CompilerParams(collective_id=1, has_side_effects=True, vmem_limit_bytes=GRANT_LATE),
         )(*g[late], *w[late], *m[late], *v[late], total)
         second = put(second)

time: 178 us -> 179 us (level)
    pallas_call x1, Pallas kernels: 115 us -> 121 us  [step(): pl.pallas_call(functools.partial(early_kernel, n, (e, l)), out_shape=[*vm...]
    pallas_call x1, Pallas kernels: 57.2 us -> 52.1 us  [step(): pl.pallas_call(functools.partial(late_kernel, n, l), out_shape=vmem((*w[l...]
where the time goes in v4:
time: 179 us
  Pallas kernels  178 us (99%)
    pallas_call x1, Pallas kernels, step(): pl.pallas_call(functools.partial(early_kernel, n, (e, l)), out_shape=[*vm...  121 us
    pallas_call x1, Pallas kernels, step(): pl.pallas_call(functools.partial(late_kernel, n, l), out_shape=vmem((*w[l...  52.1 us
    pallas_call x2, Pallas kernels, put(): pl.pallas_call(functools.partial(put_kernel, count), out_shape=[pltpu.HBM...  5.64 us

profile of v4, /device:TPU:22, one launch (start us, length us, event | category | flops | bytes accessed | tf_op | source)
XLA Modules:
  0.0 178.9 jit_solution(11531532255313934947)
XLA Ops:
  0.6 120.5 %shard_map.187 = (bf16[2,512,1408]{2,1,0:T(8,128)(2,1)S(1)}, bf16[2,512,1408]{2,1,0:T(8,128)(2,1)S(1)}, f32[2,64,1408]{2,1,0:T(8,128)S(1)}, f32[2,64,1408]{2,1,0...) custom-call(bf16[1,2,512,1408]{3,2,1,0:T(8,128)(2,1)} %refs_0_.2, ...), custom_call_target="tpu_custom_call" | custom-call | tf_op jit(solution)/shard_map/pallas_call | solution.py:339
  121.2 3.6 %shard_map.188 = (bf16[2,512,1408]{2,1,0:T(8,128)(2,1)}, bf16[2,512,1408]{2,1,0:T(8,128)(2,1)}, f32[2,64,1408]{2,1,0:T(8,128)}, f32[2,64,1408]{2,1,0:T(8,128)}, ...) custom-call(bf16[2,512,1408]{2,1,0:T(8,128)(2,1)S(1)} %get-tuple-element.29.refs_0_, ...), custom_call_target="tpu_custom_call" | custom-call | tf_op jit(solution)/shard_map/pallas_call | solution.py:318
  124.8 52.1 %shard_map.189 = (bf16[2,1408,512]{2,1,0:T(8,128)(2,1)S(1)}, f32[2,176,512]{2,1,0:T(8,128)S(1)}, f32[2,176,512]{2,1,0:T(8,128)S(1)}) custom-call(bf16[1,2,1408,512]{3,2,1,0:T(8,128)(2,1)} %refs_0_.3, bf16[2,1408,512]{2,1,0:T(8,128)(2,1)} %refs_1_.3, f32[2,176,512]{2,1,0:T(8,128)} %refs_2_.3, f32[2,176,512]{2,1,0:T(8,128)} %refs_3_.3, ...), custom_call_target="tpu_custom_call" | custom-call | tf_op jit(solution)/shard_map/pallas_call | solution.py:353
  176.8 2.1 %shard_map.190 = (bf16[2,1408,512]{2,1,0:T(8,128)(2,1)}, f32[2,176,512]{2,1,0:T(8,128)}, f32[2,176,512]{2,1,0:T(8,128)}) custom-call(bf16[2,1408,512]{2,1,0:T(8,128)(2,1)S(1)} %get-tuple-element.39.refs_0_, f32[2,176,512]{2,1,0:T(8,128)S(1)} %get-tuple-element.40.refs_1_, f32[2,176,512]{2,1,0:T(8,128)S(1)} %get-tuple-element.41.refs_2_), custom_call_target="tpu_custom_call" | custom-call | tf_op jit(solution)/shard_map/pallas_call | solution.py:318

commit v5 on v4

--- a/solution.py
+++ b/solution.py
@@ -292,16 +292,12 @@
         copy.start()
         copy.wait()
 
-    @pl.when(even())
-    def _():
-        ring.pass_on()
-        for p in range(ring.pieces):
-            ring.finish_sum(p)
-        ring.sums_sent()
-
+    pl.when(even())(ring.pass_on)
     for p in range(ring.pieces):
+        pl.when(even())(functools.partial(ring.finish_sum, p))
         ring.step(p)
     ring.gather()
+    pl.when(even())(ring.sums_sent)
 
 
 def put_kernel(count, *refs):

time: 179 us -> 179 us (level)
  no operation moved by 1% of the time
where the time goes in v5:
time: 179 us; the launch traced here: 178 us
  Pallas kernels  177 us (99%)
    pallas_call x1, Pallas kernels, step(): pl.pallas_call(functools.partial(early_kernel, n, (e, l)), out_shape=[*vm...  121 us
    pallas_call x1, Pallas kernels, step(): pl.pallas_call(functools.partial(late_kernel, n, l), out_shape=vmem((*w[l...  51.2 us
    pallas_call x2, Pallas kernels, put(): pl.pallas_call(functools.partial(put_kernel, count), out_shape=[pltpu.HBM...  5.64 us

profile of v5, /device:TPU:22, one launch (start us, length us, event | category | flops | bytes accessed | tf_op | source)
XLA Modules:
  0.0 178.0 jit_solution(7128941488329648907)
XLA Ops:
  0.6 120.5 %shard_map.187 = (bf16[2,512,1408]{2,1,0:T(8,128)(2,1)S(1)}, bf16[2,512,1408]{2,1,0:T(8,128)(2,1)S(1)}, f32[2,64,1408]{2,1,0:T(8,128)S(1)}, f32[2,64,1408]{2,1,0...) custom-call(bf16[1,2,512,1408]{3,2,1,0:T(8,128)(2,1)} %refs_0_.2, ...), custom_call_target="tpu_custom_call" | custom-call | tf_op jit(solution)/shard_map/pallas_call | solution.py:335
  121.2 3.6 %shard_map.188 = (bf16[2,512,1408]{2,1,0:T(8,128)(2,1)}, bf16[2,512,1408]{2,1,0:T(8,128)(2,1)}, f32[2,64,1408]{2,1,0:T(8,128)}, f32[2,64,1408]{2,1,0:T(8,128)}, ...) custom-call(bf16[2,512,1408]{2,1,0:T(8,128)(2,1)S(1)} %get-tuple-element.29.refs_0_, ...), custom_call_target="tpu_custom_call" | custom-call | tf_op jit(solution)/shard_map/pallas_call | solution.py:314
  124.8 51.2 %shard_map.189 = (bf16[2,1408,512]{2,1,0:T(8,128)(2,1)S(1)}, f32[2,176,512]{2,1,0:T(8,128)S(1)}, f32[2,176,512]{2,1,0:T(8,128)S(1)}) custom-call(bf16[1,2,1408,512]{3,2,1,0:T(8,128)(2,1)} %refs_0_.3, bf16[2,1408,512]{2,1,0:T(8,128)(2,1)} %refs_1_.3, f32[2,176,512]{2,1,0:T(8,128)} %refs_2_.3, f32[2,176,512]{2,1,0:T(8,128)} %refs_3_.3, ...), custom_call_target="tpu_custom_call" | custom-call | tf_op jit(solution)/shard_map/pallas_call | solution.py:349
  175.9 2.1 %shard_map.190 = (bf16[2,1408,512]{2,1,0:T(8,128)(2,1)}, f32[2,176,512]{2,1,0:T(8,128)}, f32[2,176,512]{2,1,0:T(8,128)}) custom-call(bf16[2,1408,512]{2,1,0:T(8,128)(2,1)S(1)} %get-tuple-element.39.refs_0_, f32[2,176,512]{2,1,0:T(8,128)S(1)} %get-tuple-element.40.refs_1_, f32[2,176,512]{2,1,0:T(8,128)S(1)} %get-tuple-element.41.refs_2_), custom_call_target="tpu_custom_call" | custom-call | tf_op jit(solution)/shard_map/pallas_call | solution.py:314

commit v6 on v5

v6 whole, which is shorter than its diff:
```python
import functools

import jax
import jax.numpy as jnp
from jax import lax
from jax.experimental import pallas as pl
from jax.experimental.pallas import tpu as pltpu
from jax.sharding import PartitionSpec as P

MESH = pl.DeviceIdType.MESH
DMA = pltpu.SemaphoreType.DMA
HBM, VMEM = pl.BlockSpec(memory_space=pltpu.HBM), pl.BlockSpec(memory_space=pltpu.VMEM)
ROWS = 16
EARLY_PIECES, LATE_PIECES = 1, 3
GRANT_EARLY, GRANT_LATE = 57_000_000, 61_500_000


def adamw(w, m, v, g):
    m = 0.9 * m + 0.1 * g
    v = 0.95 * v + 0.05 * g * g
    step = m * lax.rsqrt(v + 1e-8) + 0.1 * w
    return (w - 0.02 * step).astype(jnp.bfloat16), m, v


def by_rows(count, body):
    lax.fori_loop(0, count // ROWS, lambda i, _: body(pl.multiple_of(i * ROWS, ROWS)), None)


class Ring:
    def __init__(self, n, me, shape, pieces, g, w, m, v, results, buffers, sems):
        self.n, self.me, self.g, self.w, self.m, self.v = n, me, g, w, m, v
        self.w_out, self.m_out, self.v_out = results
        self.terms, self.inbox, self.total, self.own, self.m_in, self.v_in = buffers
        self.load_sem, self.state_sem, self.send_sem, self.recv_sem = sems
        self.to = [lax.rem(me + 1, n), lax.rem(me + n - 1, n)]
        weights, self.layers, self.block_rows, _ = shape
        self.parts, self.hops, self.place, _, self.message, _ = self.cut(n, pieces, shape)
        self.pieces = len(self.parts)
        self.far = n // 2
        self.loads_over = set()

    @staticmethod
    def cut(n, pieces, shape):
        weights, layers, rows, _ = shape
        size = -(-rows // (pieces * ROWS)) * ROWS
        parts, hops, place, message = [], [], {}, {}
        end = [0, 0]
        for k in range(weights):
            for layer in range(layers):
                for i, r in enumerate(range(0, rows, size)):
                    p, count = len(parts), min(size, rows - r)
                    parts.append((k, layer, r, count))
                    ways = (n // 2, (n - 1) // 2)
                    hops.append(ways if (i + layer) % 2 == 0 else ways[::-1])
                    for s in (0, 1):
                        for left in range(1, hops[p][s] + 1):
                            place[p, s, left] = end[s]
                            end[s] += count
                            message[p, s, left] = len(message)
        assert end[0] == end[1]
        return parts, hops, place, end[0], message, len(message)

    @classmethod
    def scratch(cls, n, pieces, shape, state):
        weights, layers, rows, columns = shape
        _, _, _, inbox_rows, _, messages = cls.cut(n, pieces, shape)
        whole = (weights * layers, rows, columns)
        data = [pltpu.VMEM((n, *whole), jnp.bfloat16), pltpu.VMEM((2, inbox_rows, columns), jnp.bfloat16)]
        if state:
            data += [pltpu.VMEM(whole, t) for t in (jnp.bfloat16, jnp.bfloat16, jnp.float32, jnp.float32)]
        return [*data, DMA((n,)), DMA((3,)), DMA((2,)), DMA((messages,))]

    def at(self, away):
        return lax.rem(self.me + (away + self.n), self.n)

    def block(self, owner):
        return pl.ds(pl.multiple_of(owner * self.block_rows, self.block_rows), self.block_rows)

    def rows(self, p, owner):
        _, _, first, count = self.parts[p]
        return pl.ds(pl.multiple_of(owner * self.block_rows + first, ROWS), count)

    def matrix(self, p):
        k, layer, *_ = self.parts[p]
        return k * self.layers + layer

    def term(self, p, away):
        _, _, first, count = self.parts[p]
        return self.terms.at[away % self.n, self.matrix(p), pl.ds(first, count)]

    def came(self, p, side, left):
        return self.inbox.at[side, pl.ds(self.place[p, side, left], self.parts[p][3])]

    def load_terms(self):
        for left in range(self.far - 1, -1, -1):
            for away in sorted({left, -left}):
                for k, g in enumerate(self.g):
                    target = self.terms.at[away % self.n, pl.ds(k * self.layers, self.layers)]
                    pltpu.make_async_copy(g.at[0, :, self.block(self.at(away))], target, self.load_sem.at[away % self.n]).start()

    def loaded(self, away):
        if away not in self.loads_over:
            self.loads_over.add(away)
            whole = self.terms.at[away % self.n]
            pltpu.make_async_copy(whole, whole, self.load_sem.at[away % self.n]).wait()

    def load_states(self):
        for k in range(len(self.g)):
            mine = pl.ds(k * self.layers, self.layers)
            sources = (self.w[k].at[:, self.block(self.me)], self.m[k], self.v[k])
            for i, (source, target) in enumerate(zip(sources, (self.own, self.m_in, self.v_in), strict=True)):
                pltpu.make_async_copy(source, target.at[mine], self.state_sem.at[i]).start()

    def states_loaded(self):
        for i, whole in enumerate((self.own, self.m_in, self.v_in)):
            pltpu.make_async_copy(whole, whole, self.state_sem.at[i]).wait()

    def remote(self, side, source, target, recv_sem):
        return pltpu.make_async_remote_copy(
            src_ref=source,
            dst_ref=target,
            send_sem=self.send_sem.at[side],
            recv_sem=self.recv_sem.at[recv_sem],
            device_id={"dp": self.to[side]},
            device_id_type=MESH,
        )

    def sum_copy(self, p, side, left):
        away = left if side == 0 else -left
        if self.hops[p][side] == left:
            k, layer, *_ = self.parts[p]
            source = self.g[k].at[0, layer, self.rows(p, self.at(away))]
        else:
            source = self.term(p, away)
        return self.remote(side, source, self.came(p, side, left), self.message[p, side, left])

    def gather_copy(self, p, side, hop, back):
        away = hop - back
        k, layer, *_ = self.parts[p]
        block = self.w_out[k].at[layer, self.rows(p, self.at(-away if side == 0 else away))]
        return self.remote(side, block, block, self.message[p, side, self.hops[p][side] + 1 - hop])

    def live(self, side, hops):
        return [p for p in range(self.pieces) if self.hops[p][side] >= hops]

    def first_terms(self):
        for left in range(self.far, 0, -1):
            for order in zip(*([p for p in range(self.pieces) if self.hops[p][s] == left] for s in (0, 1)), strict=True):
                for s, p in enumerate(order):
                    self.sum_copy(p, s, left).start()

    def pass_on(self):
        for left in range(self.far - 1, 0, -1):
            for order in zip(*(self.live(s, left + 1) for s in (0, 1)), strict=True):
                for s, p in enumerate(order):
                    away = left if s == 0 else -left
                    self.loaded(away)
                    self.sum_copy(p, s, left + 1).wait_recv()
                    here, came = self.term(p, away), self.came(p, s, left + 1)

                    def add(r, here=here, came=came):
                        r = pl.ds(r, ROWS)
                        here[r, :] = (here[r, :].astype(jnp.float32) + came[r, :].astype(jnp.float32)).astype(jnp.bfloat16)

                    by_rows(self.parts[p][3], add)
                    self.sum_copy(p, s, left).start()

    def finish_sum(self, p):
        self.loaded(0)
        for s in (0, 1):
            self.sum_copy(p, s, 1).wait_recv()
        _, _, first, count = self.parts[p]

        def add(r):
            here = pl.ds(r, ROWS)
            parts = [ref[here, :].astype(jnp.float32) for ref in (self.term(p, 0), self.came(p, 0, 1), self.came(p, 1, 1))]
            self.total.at[self.matrix(p)][pl.ds(first + r, ROWS), :] = (parts[0] + parts[1] + parts[2]).astype(jnp.bfloat16)

        by_rows(count, add)

    def step(self, p):
        k, layer, first, count = self.parts[p]

        def take(r):
            rows = pl.ds(first + r, ROWS)
            w, m, v, g = (ref.at[self.matrix(p)][rows, :] for ref in (self.own, self.m_in, self.v_in, self.total))
            new = adamw(w.astype(jnp.float32), m, v, g.astype(jnp.float32))
            self.w_out[k].at[layer][pl.ds(pl.multiple_of(self.me * self.block_rows + (first + r), ROWS), ROWS), :] = new[0]
            self.m_out[k].at[layer][rows, :] = new[1]
            self.v_out[k].at[layer][rows, :] = new[2]

        by_rows(count, take)
        for s in (0, 1):
            self.gather_copy(p, s, 1, 1).start()

    def gather(self):
        for hop in range(2, self.far + 1):
            order = [self.live(s, hop) for s in (0, 1)]
            for s in (0, 1):
                if hop == self.far - 1:
                    order[s].sort(key=lambda p, s=s: -self.hops[p][s])
            for pair in zip(*order, strict=True):
                for s, p in enumerate(pair):
                    self.gather_copy(p, s, hop - 1, 0).wait_recv()
                    self.gather_copy(p, s, hop, 1).start()
        for hop in (self.far - 1, self.far):
            for p in range(self.pieces):
                for s in (0, 1):
                    if self.hops[p][s] == hop:
                        self.gather_copy(p, s, hop, 0).wait_recv()

    def all_sent(self, phases):
        for s in (0, 1):
            whole = self.inbox if phases == 2 else self.inbox.at[s]
            pltpu.make_async_copy(whole, whole, self.send_sem.at[s]).wait()

    def greet(self):
        barrier = pltpu.get_barrier_semaphore()
        for neighbour in self.to:
            pl.semaphore_signal(barrier, inc=1, device_id={"dp": neighbour}, device_id_type=MESH)
        pl.semaphore_wait(barrier, 2)


def odd():
    return lax.rem(lax.axis_index("rep"), 2) == 1


def even():
    return lax.rem(lax.axis_index("rep"), 2) == 0


def early_kernel(n, shape, late_shape, *refs):
    refs = list(refs)
    take = lambda c: [refs.pop(0) for _ in range(c)]
    e, l = shape[0], late_shape[0]
    g, w, m, v, late_g = take(e), take(e), take(e), take(e), take(l)
    results, late_total = [take(e) for _ in range(3)], refs.pop(0)
    me = lax.axis_index("dp")
    ring = Ring(n, me, shape, EARLY_PIECES, g, w, m, v, results, take(6), take(4))
    held = (*take(2), late_total, None, None, None)
    late = Ring(n, me, late_shape, LATE_PIECES, late_g, None, None, None, (None,) * 3, held, take(4))

    ring.greet()

    @pl.when(odd())
    def _():
        late.first_terms()

    ring.first_terms()

    @pl.when(odd())
    def _():
        late.load_terms()

    ring.load_terms()
    ring.load_states()

    @pl.when(odd())
    def _():
        late.pass_on()
        for p in range(late.pieces):
            late.finish_sum(p)

    ring.pass_on()
    ring.states_loaded()
    for p in range(ring.pieces):
        ring.finish_sum(p)
        ring.step(p)
    ring.gather()
    ring.all_sent(2)
    pl.when(odd())(functools.partial(late.all_sent, 1))


def late_kernel(n, shape, *refs):
    refs = list(refs)
    take = lambda c: [refs.pop(0) for _ in range(c)]
    count = shape[0]
    g, w, m, v, total = take(count), take(count), take(count), take(count), refs.pop(0)
    results = [take(count) for _ in range(3)]
    ring = Ring(n, lax.axis_index("dp"), shape, LATE_PIECES, g, w, m, v, results, take(6), take(4))
    total_sem = refs.pop(0)
    ring.greet()

    @pl.when(even())
    def _():
        ring.first_terms()
        ring.load_terms()

    ring.load_states()

    @pl.when(odd())
    def _():
        copy = pltpu.make_async_copy(total, ring.total, total_sem)
        copy.start()
        copy.wait()

    pl.when(even())(ring.pass_on)
    ring.states_loaded()
    pl.when(even())(functools.partial(ring.loaded, 0))
    for p in range(ring.pieces):
        pl.when(even())(functools.partial(ring.finish_sum, p))
        ring.step(p)
    ring.gather()
    pl.when(even())(functools.partial(ring.all_sent, 2))
    pl.when(odd())(functools.partial(ring.all_sent, 1))


def put_kernel(count, *refs):
    sources, results, sem = refs[:count], refs[count:-1], refs[-1]
    copies = [pltpu.make_async_copy(a, b, sem.at[i]) for i, (a, b) in enumerate(zip(sources, results, strict=True))]
    for copy in copies:
        copy.start()
    for copy in copies:
        copy.wait()


def put(arrays):
    count = len(arrays)
    return pl.pallas_call(
        functools.partial(put_kernel, count),
        out_shape=[pltpu.HBM(one.shape, one.dtype) for one in arrays],
        in_specs=[VMEM] * count,
        out_specs=[HBM] * count,
        scratch_shapes=[DMA((count,))],
        compiler_params=pltpu.CompilerParams(vmem_limit_bytes=1 << 20),
    )(*arrays)


def solution(mesh):
    n = mesh.shape["dp"]

    def step(*arrays):
        g, w, m, v = (arrays[i : i + 3] for i in (0, 3, 6, 9))
        early, late = slice(0, 2), slice(2, 3)
        e, l = len(g[early]), len(g[late])
        vmem = lambda several: [pltpu.VMEM(one.shape, one.dtype) for one in several]
        early_shape, late_shape = (e, *m[early][0].shape), (l, *m[late][0].shape)

        *first, total = pl.pallas_call(
            functools.partial(early_kernel, n, early_shape, late_shape),
            out_shape=[*vmem((*w[early], *m[early], *v[early])), pltpu.VMEM((l * late_shape[1], *late_shape[2:]), jnp.bfloat16)],
            in_specs=[HBM] * (4 * e + l),
            out_specs=[VMEM] * (3 * e + 1),
            scratch_shapes=[
                *Ring.scratch(n, EARLY_PIECES, early_shape, True),
                *Ring.scratch(n, LATE_PIECES, late_shape, False),
            ],
            compiler_params=pltpu.CompilerParams(collective_id=0, has_side_effects=True, vmem_limit_bytes=GRANT_EARLY),
        )(*g[early], *w[early], *m[early], *v[early], *g[late])
        *first, total = put([*first, total])
        second = pl.pallas_call(
            functools.partial(late_kernel, n, late_shape),
            out_shape=vmem((*w[late], *m[late], *v[late])),
            in_specs=[HBM] * (4 * l + 1),
            out_specs=[VMEM] * (3 * l),
            scratch_shapes=[*Ring.scratch(n, LATE_PIECES, late_shape, True), DMA],
            compiler_params=pltpu.CompilerParams(collective_id=1, has_side_effects=True, vmem_limit_bytes=GRANT_LATE),
        )(*g[late], *w[late], *m[late], *v[late], total)
        second = put(second)
        return tuple(one for i in range(3) for one in (*first[i * e : (i + 1) * e], *second[i * l : (i + 1) * l]))

    all_of, cut = P(None, None, None), P(None, "dp", None)
    return jax.shard_map(
        step,
        mesh=mesh,
        in_specs=(P(("rep", "dp"), None, None, None),) * 3 + (all_of,) * 3 + (cut,) * 6,
        out_specs=(P("rep", None, None),) * 3 + (P("rep", "dp", None),) * 6,
        check_vma=False,
    )
```

time: 179 us -> 176 us (0.983)
  Pallas kernels: 177 us -> 174 us
    pallas_call x2, Pallas kernels: 172 us -> 169 us  [the longest x1 116 us: step(): pl.pallas_call(functools.partial(early_kernel, n, early_shape, late_shape...]
where the time goes in v6:
time: 176 us; the launch traced here: 175 us
  Pallas kernels  174 us (99%)
    pallas_call x1, Pallas kernels, step(): pl.pallas_call(functools.partial(early_kernel, n, early_shape, late_shape...  116 us
    pallas_call x1, Pallas kernels, step(): pl.pallas_call(functools.partial(late_kernel, n, late_shape), out_shape=v...  53.3 us
    pallas_call x2, Pallas kernels, put(): pl.pallas_call(functools.partial(put_kernel, count), out_shape=[pltpu.HBM...  5.64 us

profile of v6, /device:TPU:22, one launch (start us, length us, event | category | flops | bytes accessed | tf_op | source)
XLA Modules:
  0.0 175.1 jit_solution(6304014293230817287)
XLA Ops:
  0.6 115.5 %shard_map.187 = (bf16[2,512,1408]{2,1,0:T(8,128)(2,1)S(1)}, bf16[2,512,1408]{2,1,0:T(8,128)(2,1)S(1)}, f32[2,64,1408]{2,1,0:T(8,128)S(1)}, f32[2,64,1408]{2,1,0...) custom-call(bf16[1,2,512,1408]{3,2,1,0:T(8,128)(2,1)} %refs_0_.2, ...), custom_call_target="tpu_custom_call" | custom-call | tf_op jit(solution)/shard_map/pallas_call | solution.py:339
  116.2 3.6 %shard_map.188 = (bf16[2,512,1408]{2,1,0:T(8,128)(2,1)}, bf16[2,512,1408]{2,1,0:T(8,128)(2,1)}, f32[2,64,1408]{2,1,0:T(8,128)}, f32[2,64,1408]{2,1,0:T(8,128)}, ...) custom-call(bf16[2,512,1408]{2,1,0:T(8,128)(2,1)S(1)} %get-tuple-element.29.refs_0_, ...), custom_call_target="tpu_custom_call" | custom-call | tf_op jit(solution)/shard_map/pallas_call | solution.py:319
  119.7 53.3 %shard_map.189 = (bf16[2,1408,512]{2,1,0:T(8,128)(2,1)S(1)}, f32[2,176,512]{2,1,0:T(8,128)S(1)}, f32[2,176,512]{2,1,0:T(8,128)S(1)}) custom-call(bf16[1,2,1408,512]{3,2,1,0:T(8,128)(2,1)} %refs_0_.3, bf16[2,1408,512]{2,1,0:T(8,128)(2,1)} %refs_1_.3, f32[2,176,512]{2,1,0:T(8,128)} %refs_2_.3, f32[2,176,512]{2,1,0:T(8,128)} %refs_3_.3, ...), custom_call_target="tpu_custom_call" | custom-call | tf_op jit(solution)/shard_map/pallas_call | solution.py:351
  173.0 2.1 %shard_map.190 = (bf16[2,1408,512]{2,1,0:T(8,128)(2,1)}, f32[2,176,512]{2,1,0:T(8,128)}, f32[2,176,512]{2,1,0:T(8,128)}) custom-call(bf16[2,1408,512]{2,1,0:T(8,128)(2,1)S(1)} %get-tuple-element.39.refs_0_, f32[2,176,512]{2,1,0:T(8,128)S(1)} %get-tuple-element.40.refs_1_, f32[2,176,512]{2,1,0:T(8,128)S(1)} %get-tuple-element.41.refs_2_), custom_call_target="tpu_custom_call" | custom-call | tf_op jit(solution)/shard_map/pallas_call | solution.py:319

commit v7 on v6

--- a/solution.py
+++ b/solution.py
@@ -11,7 +11,7 @@
 DMA = pltpu.SemaphoreType.DMA
 HBM, VMEM = pl.BlockSpec(memory_space=pltpu.HBM), pl.BlockSpec(memory_space=pltpu.VMEM)
 ROWS = 16
-EARLY_PIECES, LATE_PIECES = 1, 3
+EARLY_PIECES, LATE_PIECES = 1, 4
 GRANT_EARLY, GRANT_LATE = 57_000_000, 61_500_000
 
 
@@ -222,11 +222,11 @@
 
 
 def odd():
+    return lax.rem(lax.axis_index("rep"), 2) == 0
+
+
+def even():
     return lax.rem(lax.axis_index("rep"), 2) == 1
-
-
-def even():
-    return lax.rem(lax.axis_index("rep"), 2) == 0
 
 
 def early_kernel(n, shape, late_shape, *refs):
@@ -279,6 +279,9 @@
     results = [take(count) for _ in range(3)]
     ring = Ring(n, lax.axis_index("dp"), shape, LATE_PIECES, g, w, m, v, results, take(6), take(4))
     total_sem = refs.pop(0)
+    ring.load_states()
+    total_copy = pltpu.make_async_copy(total, ring.total, total_sem)
+    pl.when(odd())(total_copy.start)
     ring.greet()
 
     @pl.when(even())
@@ -286,14 +289,7 @@
         ring.first_terms()
         ring.load_terms()
 
-    ring.load_states()
-
-    @pl.when(odd())
-    def _():
-        copy = pltpu.make_async_copy(total, ring.total, total_sem)
-        copy.start()
-        copy.wait()
-
+    pl.when(odd())(total_copy.wait)
     pl.when(even())(ring.pass_on)
     ring.states_loaded()
     pl.when(even())(functools.partial(ring.loaded, 0))

time: 176 us -> 175 us (level)
    pallas_call x1, Pallas kernels: 53.3 us -> 28 us  [step(): pl.pallas_call(functools.partial(late_kernel, n, late_shape), out_shape=v...]
    pallas_call x1, Pallas kernels: 116 us -> 140 us  [step(): pl.pallas_call(functools.partial(early_kernel, n, early_shape, late_shape...]
where the time goes in v7:
time: 175 us
  Pallas kernels  174 us (99%)
    pallas_call x1, Pallas kernels, step(): pl.pallas_call(functools.partial(early_kernel, n, early_shape, late_shape...  140 us
    pallas_call x1, Pallas kernels, step(): pl.pallas_call(functools.partial(late_kernel, n, late_shape), out_shape=v...  28 us
    pallas_call x2, Pallas kernels, put(): pl.pallas_call(functools.partial(put_kernel, count), out_shape=[pltpu.HBM...  5.64 us

profile of v7, /device:TPU:22, one launch (start us, length us, event | category | flops | bytes accessed | tf_op | source)
XLA Modules:
  0.0 174.7 jit_solution(6158813120332974355)
XLA Ops:
  0.6 140.5 %shard_map.187 = (bf16[2,512,1408]{2,1,0:T(8,128)(2,1)S(1)}, bf16[2,512,1408]{2,1,0:T(8,128)(2,1)S(1)}, f32[2,64,1408]{2,1,0:T(8,128)S(1)}, f32[2,64,1408]{2,1,0...) custom-call(bf16[1,2,512,1408]{3,2,1,0:T(8,128)(2,1)} %refs_0_.2, ...), custom_call_target="tpu_custom_call" | custom-call | tf_op jit(solution)/shard_map/pallas_call | solution.py:335
  141.1 3.6 %shard_map.188 = (bf16[2,512,1408]{2,1,0:T(8,128)(2,1)}, bf16[2,512,1408]{2,1,0:T(8,128)(2,1)}, f32[2,64,1408]{2,1,0:T(8,128)}, f32[2,64,1408]{2,1,0:T(8,128)}, ...) custom-call(bf16[2,512,1408]{2,1,0:T(8,128)(2,1)S(1)} %get-tuple-element.29.refs_0_, ...), custom_call_target="tpu_custom_call" | custom-call | tf_op jit(solution)/shard_map/pallas_call | solution.py:315
  144.7 28.0 %shard_map.189 = (bf16[2,1408,512]{2,1,0:T(8,128)(2,1)S(1)}, f32[2,176,512]{2,1,0:T(8,128)S(1)}, f32[2,176,512]{2,1,0:T(8,128)S(1)}) custom-call(bf16[1,2,1408,512]{3,2,1,0:T(8,128)(2,1)} %refs_0_.3, bf16[2,1408,512]{2,1,0:T(8,128)(2,1)} %refs_1_.3, f32[2,176,512]{2,1,0:T(8,128)} %refs_2_.3, f32[2,176,512]{2,1,0:T(8,128)} %refs_3_.3, ...), custom_call_target="tpu_custom_call" | custom-call | tf_op jit(solution)/shard_map/pallas_call | solution.py:347
  172.7 2.1 %shard_map.190 = (bf16[2,1408,512]{2,1,0:T(8,128)(2,1)}, f32[2,176,512]{2,1,0:T(8,128)}, f32[2,176,512]{2,1,0:T(8,128)}) custom-call(bf16[2,1408,512]{2,1,0:T(8,128)(2,1)S(1)} %get-tuple-element.39.refs_0_, f32[2,176,512]{2,1,0:T(8,128)S(1)} %get-tuple-element.40.refs_1_, f32[2,176,512]{2,1,0:T(8,128)S(1)} %get-tuple-element.41.refs_2_), custom_call_target="tpu_custom_call" | custom-call | tf_op jit(solution)/shard_map/pallas_call | solution.py:315

commit v8 on v7

--- a/solution.py
+++ b/solution.py
@@ -12,7 +12,7 @@
 HBM, VMEM = pl.BlockSpec(memory_space=pltpu.HBM), pl.BlockSpec(memory_space=pltpu.VMEM)
 ROWS = 16
 EARLY_PIECES, LATE_PIECES = 1, 4
-GRANT_EARLY, GRANT_LATE = 57_000_000, 61_500_000
+GRANT_EARLY, GRANT_LATE = 54_000_000, 61_500_000
 
 
 def adamw(w, m, v, g):
@@ -34,7 +34,7 @@
         self.load_sem, self.state_sem, self.send_sem, self.recv_sem = sems
         self.to = [lax.rem(me + 1, n), lax.rem(me + n - 1, n)]
         weights, self.layers, self.block_rows, _ = shape
-        self.parts, self.hops, self.place, _, self.message, _ = self.cut(n, pieces, shape)
+        self.parts, self.hops, self.place, self.inbox_rows, self.message, _ = self.cut(n, pieces, shape)
         self.pieces = len(self.parts)
         self.far = n // 2
         self.loads_over = set()
@@ -61,13 +61,12 @@
         return parts, hops, place, end[0], message, len(message)
 
     @classmethod
-    def scratch(cls, n, pieces, shape, state):
+    def scratch(cls, n, pieces, shape):
         weights, layers, rows, columns = shape
         _, _, _, inbox_rows, _, messages = cls.cut(n, pieces, shape)
         whole = (weights * layers, rows, columns)
-        data = [pltpu.VMEM((n, *whole), jnp.bfloat16), pltpu.VMEM((2, inbox_rows, columns), jnp.bfloat16)]
-        if state:
-            data += [pltpu.VMEM(whole, t) for t in (jnp.bfloat16, jnp.bfloat16, jnp.float32, jnp.float32)]
+        data = [pltpu.VMEM((n, *whole), jnp.bfloat16), pltpu.VMEM((2 * inbox_rows, columns), jnp.bfloat16)]
+        data += [pltpu.VMEM(whole, t) for t in (jnp.bfloat16, jnp.bfloat16, jnp.float32, jnp.float32)]
         return [*data, DMA((n,)), DMA((3,)), DMA((2,)), DMA((messages,))]
 
     def at(self, away):
@@ -89,7 +88,7 @@
         return self.terms.at[away % self.n, self.matrix(p), pl.ds(first, count)]
 
     def came(self, p, side, left):
-        return self.inbox.at[side, pl.ds(self.place[p, side, left], self.parts[p][3])]
+        return self.inbox.at[pl.ds(side * self.inbox_rows + self.place[p, side, left], self.parts[p][3])]
 
     def load_terms(self):
         for left in range(self.far - 1, -1, -1):
@@ -134,11 +133,11 @@
             source = self.term(p, away)
         return self.remote(side, source, self.came(p, side, left), self.message[p, side, left])
 
-    def gather_copy(self, p, side, hop, back):
+    def gather_copy(self, p, side, hop, back, done=None):
         away = hop - back
         k, layer, *_ = self.parts[p]
-        block = self.w_out[k].at[layer, self.rows(p, self.at(-away if side == 0 else away))]
-        return self.remote(side, block, block, self.message[p, side, self.hops[p][side] + 1 - hop])
+        block = (layer, self.rows(p, self.at(-away if side == 0 else away)))
+        return self.remote(side, (done or self.w_out)[k].at[block], self.w_out[k].at[block], self.message[p, side, self.hops[p][side] + 1 - hop])
 
     def live(self, side, hops):
         return [p for p in range(self.pieces) if self.hops[p][side] >= hops]
@@ -166,7 +165,6 @@
                     self.sum_copy(p, s, left).start()
 
     def finish_sum(self, p):
-        self.loaded(0)
         for s in (0, 1):
             self.sum_copy(p, s, 1).wait_recv()
         _, _, first, count = self.parts[p]
@@ -193,25 +191,35 @@
         for s in (0, 1):
             self.gather_copy(p, s, 1, 1).start()
 
-    def gather(self):
-        for hop in range(2, self.far + 1):
-            order = [self.live(s, hop) for s in (0, 1)]
-            for s in (0, 1):
-                if hop == self.far - 1:
-                    order[s].sort(key=lambda p, s=s: -self.hops[p][s])
-            for pair in zip(*order, strict=True):
-                for s, p in enumerate(pair):
+    def take_steps(self):
+        self.loaded(0)
+        self.states_loaded()
+        for p in range(self.pieces):
+            self.finish_sum(p)
+            self.step(p)
+
+    def spread(self, hop, done=None):
+        order = [self.live(s, hop) for s in (0, 1)]
+        for s in (0, 1):
+            if hop == self.far - 1:
+                order[s].sort(key=lambda p, s=s: -self.hops[p][s])
+        for pair in zip(*order, strict=True):
+            for s, p in enumerate(pair):
+                if done is None:
                     self.gather_copy(p, s, hop - 1, 0).wait_recv()
-                    self.gather_copy(p, s, hop, 1).start()
-        for hop in (self.far - 1, self.far):
+                self.gather_copy(p, s, hop, 1, done).start()
+
+    def gathered(self, hops):
+        for hop in range(1, hops + 1):
             for p in range(self.pieces):
                 for s in (0, 1):
-                    if self.hops[p][s] == hop:
+                    if min(self.hops[p][s], hops) == hop:
                         self.gather_copy(p, s, hop, 0).wait_recv()
 
-    def all_sent(self, phases):
+    def all_sent(self, hops, sums):
         for s in (0, 1):
-            whole = self.inbox if phases == 2 else self.inbox.at[s]
+            rows = sum(self.parts[p][3] for hop in hops for p in self.live(s, hop)) + sums * self.inbox_rows
+            whole = self.inbox.at[pl.ds(0, rows)]
             pltpu.make_async_copy(whole, whole, self.send_sem.at[s]).wait()
 
     def greet(self):
@@ -221,105 +229,143 @@
         pl.semaphore_wait(barrier, 2)
 
 
-def odd():
+def ahead():
     return lax.rem(lax.axis_index("rep"), 2) == 0
 
 
-def even():
+def behind():
     return lax.rem(lax.axis_index("rep"), 2) == 1
+
+
+def early_hops(n):
+    return n // 2 - 2
 
 
 def early_kernel(n, shape, late_shape, *refs):
     refs = list(refs)
     take = lambda c: [refs.pop(0) for _ in range(c)]
     e, l = shape[0], late_shape[0]
-    g, w, m, v, late_g = take(e), take(e), take(e), take(e), take(l)
-    results, late_total = [take(e) for _ in range(3)], refs.pop(0)
+    data, late_data = [take(e) for _ in range(4)], [take(l) for _ in range(4)]
+    results, late_results = [take(e) for _ in range(3)], [take(l) for _ in range(3)]
     me = lax.axis_index("dp")
-    ring = Ring(n, me, shape, EARLY_PIECES, g, w, m, v, results, take(6), take(4))
-    held = (*take(2), late_total, None, None, None)
-    late = Ring(n, me, late_shape, LATE_PIECES, late_g, None, None, None, (None,) * 3, held, take(4))
+    ring = Ring(n, me, shape, EARLY_PIECES, *data, results, take(6), take(4))
+    late = Ring(n, me, late_shape, LATE_PIECES, *late_data, late_results, take(6), take(4))
 
     ring.greet()
-
-    @pl.when(odd())
-    def _():
-        late.first_terms()
-
+    pl.when(ahead())(late.first_terms)
     ring.first_terms()
 
-    @pl.when(odd())
+    @pl.when(ahead())
     def _():
         late.load_terms()
+        late.load_states()
 
     ring.load_terms()
     ring.load_states()
 
-    @pl.when(odd())
+    @pl.when(ahead())
     def _():
         late.pass_on()
-        for p in range(late.pieces):
-            late.finish_sum(p)
+        late.take_steps()
 
     ring.pass_on()
-    ring.states_loaded()
-    for p in range(ring.pieces):
-        ring.finish_sum(p)
-        ring.step(p)
-    ring.gather()
-    ring.all_sent(2)
-    pl.when(odd())(functools.partial(late.all_sent, 1))
+    ring.take_steps()
+    for hop in range(2, ring.far + 1):
+        if hop <= early_hops(n):
+            pl.when(ahead())(functools.partial(late.spread, hop))
+        ring.spread(hop)
+    ring.gathered(ring.far)
+    ring.all_sent(range(1, ring.far + 1), True)
+
+    @pl.when(ahead())
+    def _():
+        late.gathered(early_hops(n))
+        late.all_sent(range(1, early_hops(n) + 1), True)
 
 
 def late_kernel(n, shape, *refs):
     refs = list(refs)
     take = lambda c: [refs.pop(0) for _ in range(c)]
     count = shape[0]
-    g, w, m, v, total = take(count), take(count), take(count), take(count), refs.pop(0)
+    data, done = [take(count) for _ in range(4)], take(count)
     results = [take(count) for _ in range(3)]
-    ring = Ring(n, lax.axis_index("dp"), shape, LATE_PIECES, g, w, m, v, results, take(6), take(4))
-    total_sem = refs.pop(0)
-    ring.load_states()
-    total_copy = pltpu.make_async_copy(total, ring.total, total_sem)
-    pl.when(odd())(total_copy.start)
+    ring = Ring(n, lax.axis_index("dp"), shape, LATE_PIECES, *data, results, take(6), take(4))
+    last = range(early_hops(n) + 1, ring.far + 1)
     ring.greet()
 
-    @pl.when(even())
+    @pl.when(ahead())
+    def _():
+        ring.spread(last[0], done)
+
+    @pl.when(behind())
     def _():
         ring.first_terms()
         ring.load_terms()
-
-    pl.when(odd())(total_copy.wait)
-    pl.when(even())(ring.pass_on)
-    ring.states_loaded()
-    pl.when(even())(functools.partial(ring.loaded, 0))
-    for p in range(ring.pieces):
-        pl.when(even())(functools.partial(ring.finish_sum, p))
-        ring.step(p)
-    ring.gather()
-    pl.when(even())(functools.partial(ring.all_sent, 2))
-    pl.when(odd())(functools.partial(ring.all_sent, 1))
-
-
-def put_kernel(count, *refs):
-    sources, results, sem = refs[:count], refs[count:-1], refs[-1]
-    copies = [pltpu.make_async_copy(a, b, sem.at[i]) for i, (a, b) in enumerate(zip(sources, results, strict=True))]
-    for copy in copies:
+        ring.load_states()
+        ring.pass_on()
+        ring.take_steps()
+        for hop in range(2, last[0] + 1):
+            ring.spread(hop)
+
+    for hop in last[1:]:
+        ring.spread(hop)
+    ring.gathered(ring.far)
+    pl.when(ahead())(functools.partial(ring.all_sent, last, False))
+    pl.when(behind())(functools.partial(ring.all_sent, range(1, ring.far + 1), True))
+
+
+def put_early_kernel(n, e, l, *refs):
+    refs, sem = list(refs[:-1]), refs[-1]
+    count = 3 * (e + l)
+    sources, results = refs[:count], refs[count:]
+    early = [pltpu.make_async_copy(sources[i], results[i], sem.at[i]) for i in range(3 * e)]
+    for copy in early:
         copy.start()
-    for copy in copies:
+
+    @pl.when(ahead())
+    def _():
+        reach = early_hops(n)
+        late = [pltpu.make_async_copy(sources[i], results[i], sem.at[i]) for i in range(3 * e + l, count)]
+        late += block_copies(n, sources[3 * e : 3 * e + l], results[3 * e : 3 * e + l], range(-reach, reach + 1), sem, count)
+        for copy in late:
+            copy.start()
+        for copy in late:
+            copy.wait()
+
+    for copy in early:
         copy.wait()
 
 
-def put(arrays):
-    count = len(arrays)
-    return pl.pallas_call(
-        functools.partial(put_kernel, count),
-        out_shape=[pltpu.HBM(one.shape, one.dtype) for one in arrays],
-        in_specs=[VMEM] * count,
-        out_specs=[HBM] * count,
-        scratch_shapes=[DMA((count,))],
-        compiler_params=pltpu.CompilerParams(vmem_limit_bytes=1 << 20),
-    )(*arrays)
+def block_copies(n, sources, results, aways, sem, first):
+    me = lax.axis_index("dp")
+    copies = []
+    for source, result in zip(sources, results, strict=True):
+        rows = source.shape[1] // n
+        for away in aways:
+            block = pl.ds(pl.multiple_of(lax.rem(me + (away + n), n) * rows, rows), rows)
+            copies.append(pltpu.make_async_copy(source.at[:, block], result.at[:, block], sem.at[first + len(copies)]))
+    return copies
+
+
+def put_late_kernel(n, l, *refs):
+    sources, results, sem = refs[: 3 * l], refs[6 * l : 9 * l], refs[-1]
+
+    @pl.when(ahead())
+    def _():
+        reach = early_hops(n)
+        copies = block_copies(n, sources[:l], results[:l], range(reach + 1, n - reach), sem, 3 * l)
+        for copy in copies:
+            copy.start()
+        for copy in copies:
+            copy.wait()
+
+    @pl.when(behind())
+    def _():
+        copies = [pltpu.make_async_copy(sources[i], results[i], sem.at[i]) for i in range(3 * l)]
+        for copy in copies:
+            copy.start()
+        for copy in copies:
+            copy.wait()
 
 
 def solution(mesh):
@@ -330,29 +376,44 @@
         early, late = slice(0, 2), slice(2, 3)
         e, l = len(g[early]), len(g[late])
         vmem = lambda several: [pltpu.VMEM(one.shape, one.dtype) for one in several]
+        hbm = lambda several: [pltpu.HBM(one.shape, one.dtype) for one in several]
         early_shape, late_shape = (e, *m[early][0].shape), (l, *m[late][0].shape)
-
-        *first, total = pl.pallas_call(
+        early_results, late_results = (*w[early], *m[early], *v[early]), (*w[late], *m[late], *v[late])
+
+        first = pl.pallas_call(
             functools.partial(early_kernel, n, early_shape, late_shape),
-            out_shape=[*vmem((*w[early], *m[early], *v[early])), pltpu.VMEM((l * late_shape[1], *late_shape[2:]), jnp.bfloat16)],
-            in_specs=[HBM] * (4 * e + l),
-            out_specs=[VMEM] * (3 * e + 1),
-            scratch_shapes=[
-                *Ring.scratch(n, EARLY_PIECES, early_shape, True),
-                *Ring.scratch(n, LATE_PIECES, late_shape, False),
-            ],
+            out_shape=vmem((*early_results, *late_results)),
+            in_specs=[HBM] * (4 * (e + l)),
+            out_specs=[VMEM] * (3 * (e + l)),
+            scratch_shapes=[*Ring.scratch(n, EARLY_PIECES, early_shape), *Ring.scratch(n, LATE_PIECES, late_shape)],
             compiler_params=pltpu.CompilerParams(collective_id=0, has_side_effects=True, vmem_limit_bytes=GRANT_EARLY),
-        )(*g[early], *w[early], *m[early], *v[early], *g[late])
-        *first, total = put([*first, total])
+        )(*g[early], *w[early], *m[early], *v[early], *g[late], *w[late], *m[late], *v[late])
+        first = pl.pallas_call(
+            functools.partial(put_early_kernel, n, e, l),
+            out_shape=hbm((*early_results, *late_results)),
+            in_specs=[VMEM] * (3 * (e + l)),
+            out_specs=[HBM] * (3 * (e + l)),
+            scratch_shapes=[DMA((3 * (e + l) + l * (2 * early_hops(n) + 1),))],
+            compiler_params=pltpu.CompilerParams(vmem_limit_bytes=1 << 20),
+        )(*first)
+        first, half = first[: 3 * e], first[3 * e :]
         second = pl.pallas_call(
             functools.partial(late_kernel, n, late_shape),
-            out_shape=vmem((*w[late], *m[late], *v[late])),
-            in_specs=[HBM] * (4 * l + 1),
+            out_shape=vmem(late_results),
+            in_specs=[HBM] * (5 * l),
             out_specs=[VMEM] * (3 * l),
-            scratch_shapes=[*Ring.scratch(n, LATE_PIECES, late_shape, True), DMA],
+            scratch_shapes=Ring.scratch(n, LATE_PIECES, late_shape),
             compiler_params=pltpu.CompilerParams(collective_id=1, has_side_effects=True, vmem_limit_bytes=GRANT_LATE),
-        )(*g[late], *w[late], *m[late], *v[late], total)
-        second = put(second)
+        )(*g[late], *w[late], *m[late], *v[late], *half[:l])
+        second = pl.pallas_call(
+            functools.partial(put_late_kernel, n, l),
+            out_shape=hbm(late_results),
+            in_specs=[VMEM] * (3 * l) + [HBM] * (3 * l),
+            out_specs=[HBM] * (3 * l),
+            scratch_shapes=[DMA((3 * l + l * (n - 1 - 2 * early_hops(n)),))],
+            input_output_aliases={3 * l + i: i for i in range(3 * l)},
+            compiler_params=pltpu.CompilerParams(vmem_limit_bytes=1 << 20),
+        )(*second, *half)
         return tuple(one for i in range(3) for one in (*first[i * e : (i + 1) * e], *second[i * l : (i + 1) * l]))
 
     all_of, cut = P(None, None, None), P(None, "dp", None)

time: 175 us -> 174 us (level)
    pallas_call x1, Pallas kernels: 28 us -> 15 us  [step(): pl.pallas_call(functools.partial(late_kernel, n, late_shape), out_shape=v...]
    pallas_call x1, Pallas kernels: 140 us -> 153 us  [step(): pl.pallas_call(functools.partial(early_kernel, n, early_shape, late_shape...]
where the time goes in v8:
time: 174 us
  Pallas kernels  173 us (99%)
    pallas_call x1, Pallas kernels, step(): pl.pallas_call(functools.partial(early_kernel, n, early_shape, late_shape...  153 us
    pallas_call x1, Pallas kernels, step(): pl.pallas_call(functools.partial(late_kernel, n, late_shape), out_shape=v...  15 us
    pallas_call x1, Pallas kernels, step(): pl.pallas_call(functools.partial(put_early_kernel, n, e, l), out_shape=hb...  4.51 us

profile of v8, /device:TPU:22, one launch (start us, length us, event | category | flops | bytes accessed | tf_op | source)
XLA Modules:
  0.0 174.0 jit_solution(9494598561493643337)
XLA Ops:
  0.6 152.8 %shard_map.187 = (bf16[2,512,1408]{2,1,0:T(8,128)(2,1)S(1)}, bf16[2,512,1408]{2,1,0:T(8,128)(2,1)S(1)}, f32[2,64,1408]{2,1,0:T(8,128)S(1)}, f32[2,64,1408]{2,1,0...) custom-call(bf16[1,2,512,1408]{3,2,1,0:T(8,128)(2,1)} %refs_0_.2, ...), custom_call_target="tpu_custom_call" | custom-call | tf_op jit(solution)/shard_map/pallas_call | solution.py:383
  153.4 4.5 %shard_map.188 = (bf16[2,512,1408]{2,1,0:T(8,128)(2,1)}, bf16[2,512,1408]{2,1,0:T(8,128)(2,1)}, f32[2,64,1408]{2,1,0:T(8,128)}, f32[2,64,1408]{2,1,0:T(8,128)}, ...) custom-call(bf16[2,512,1408]{2,1,0:T(8,128)(2,1)S(1)} %get-tuple-ele, ...), custom_call_target="tpu_custom_call" | custom-call | tf_op jit(solution)/shard_map/pallas_call | solution.py:391
  158.0 15.0 %shard_map.189 = (bf16[2,1408,512]{2,1,0:T(8,128)(2,1)S(1)}, f32[2,176,512]{2,1,0:T(8,128)S(1)}, f32[2,176,512]{2,1,0:T(8,128)S(1)}) custom-call(bf16[1,2,1408,512]{3,2,1,0:T(8,128)(2,1)} %refs_0_.3, bf16[2,1408,512]{2,1,0:T(8,128)(2,1)} %refs_1_.3, f32[2,176,512]{2,1,0:T(8,128)} %refs_2_.3, f32[2,176,512]{2,1,0:T(8,128)} %refs_3_.3, ...), custom_call_target="tpu_custom_call" | custom-call | tf_op jit(solution)/shard_map/pallas_call | solution.py:400
  172.9 1.0 shard_map.190

commit v9 on v8

--- a/solution.py
+++ b/solution.py
@@ -12,6 +12,7 @@
 HBM, VMEM = pl.BlockSpec(memory_space=pltpu.HBM), pl.BlockSpec(memory_space=pltpu.VMEM)
 ROWS = 16
 EARLY_PIECES, LATE_PIECES = 1, 4
+HOLD = 2400
 GRANT_EARLY, GRANT_LATE = 54_000_000, 61_500_000
 
 
@@ -295,6 +296,7 @@
 
     @pl.when(ahead())
     def _():
+        pl.delay(HOLD)
         ring.spread(last[0], done)
 
     @pl.when(behind())

time: 174 us -> 174 us (level)
  no operation moved by 1% of the time
where the time goes in v9:
time: 174 us
  Pallas kernels  173 us (99%)
    pallas_call x1, Pallas kernels, step(): pl.pallas_call(functools.partial(early_kernel, n, early_shape, late_shape...  153 us
    pallas_call x1, Pallas kernels, step(): pl.pallas_call(functools.partial(late_kernel, n, late_shape), out_shape=v...  15 us
    pallas_call x1, Pallas kernels, step(): pl.pallas_call(functools.partial(put_early_kernel, n, e, l), out_shape=hb...  4.51 us

profile of v9, /device:TPU:22, one launch (start us, length us, event | category | flops | bytes accessed | tf_op | source)
XLA Modules:
  0.0 174.0 jit_solution(9071313628370325499)
XLA Ops:
  0.6 152.8 %shard_map.187 = (bf16[2,512,1408]{2,1,0:T(8,128)(2,1)S(1)}, bf16[2,512,1408]{2,1,0:T(8,128)(2,1)S(1)}, f32[2,64,1408]{2,1,0:T(8,128)S(1)}, f32[2,64,1408]{2,1,0...) custom-call(bf16[1,2,512,1408]{3,2,1,0:T(8,128)(2,1)} %refs_0_.2, ...), custom_call_target="tpu_custom_call" | custom-call | tf_op jit(solution)/shard_map/pallas_call | solution.py:385
  153.4 4.5 %shard_map.188 = (bf16[2,512,1408]{2,1,0:T(8,128)(2,1)}, bf16[2,512,1408]{2,1,0:T(8,128)(2,1)}, f32[2,64,1408]{2,1,0:T(8,128)}, f32[2,64,1408]{2,1,0:T(8,128)}, ...) custom-call(bf16[2,512,1408]{2,1,0:T(8,128)(2,1)S(1)} %get-tuple-ele, ...), custom_call_target="tpu_custom_call" | custom-call | tf_op jit(solution)/shard_map/pallas_call | solution.py:393
  158.0 15.0 %shard_map.189 = (bf16[2,1408,512]{2,1,0:T(8,128)(2,1)S(1)}, f32[2,176,512]{2,1,0:T(8,128)S(1)}, f32[2,176,512]{2,1,0:T(8,128)S(1)}) custom-call(bf16[1,2,1408,512]{3,2,1,0:T(8,128)(2,1)} %refs_0_.3, bf16[2,1408,512]{2,1,0:T(8,128)(2,1)} %refs_1_.3, f32[2,176,512]{2,1,0:T(8,128)} %refs_2_.3, f32[2,176,512]{2,1,0:T(8,128)} %refs_3_.3, ...), custom_call_target="tpu_custom_call" | custom-call | tf_op jit(solution)/shard_map/pallas_call | solution.py:402
  172.9 1.0 shard_map.190

commit v10 on v9

--- a/solution.py
+++ b/solution.py
@@ -11,8 +11,8 @@
 DMA = pltpu.SemaphoreType.DMA
 HBM, VMEM = pl.BlockSpec(memory_space=pltpu.HBM), pl.BlockSpec(memory_space=pltpu.VMEM)
 ROWS = 16
-EARLY_PIECES, LATE_PIECES = 1, 4
-HOLD = 2400
+EARLY_PIECES, LATE_PIECES = 1, 2
+HOLD = 3200
 GRANT_EARLY, GRANT_LATE = 54_000_000, 61_500_000
 
 

time: 174 us -> 174 us (level)
  no operation moved by 1% of the time
where the time goes in v10:
time: 174 us
  Pallas kernels  173 us (99%)
    pallas_call x1, Pallas kernels, step(): pl.pallas_call(functools.partial(early_kernel, n, early_shape, late_shape...  153 us
    pallas_call x1, Pallas kernels, step(): pl.pallas_call(functools.partial(late_kernel, n, late_shape), out_shape=v...  14.7 us
    pallas_call x1, Pallas kernels, step(): pl.pallas_call(functools.partial(put_early_kernel, n, e, l), out_shape=hb...  4.51 us

profile of v10, /device:TPU:22, one launch (start us, length us, event | category | flops | bytes accessed | tf_op | source)
XLA Modules:
  0.0 173.9 jit_solution(8470058087954293146)
XLA Ops:
  0.6 153.0 %shard_map.187 = (bf16[2,512,1408]{2,1,0:T(8,128)(2,1)S(1)}, bf16[2,512,1408]{2,1,0:T(8,128)(2,1)S(1)}, f32[2,64,1408]{2,1,0:T(8,128)S(1)}, f32[2,64,1408]{2,1,0...) custom-call(bf16[1,2,512,1408]{3,2,1,0:T(8,128)(2,1)} %refs_0_.2, ...), custom_call_target="tpu_custom_call" | custom-call | tf_op jit(solution)/shard_map/pallas_call | solution.py:385
  153.7 4.5 %shard_map.188 = (bf16[2,512,1408]{2,1,0:T(8,128)(2,1)}, bf16[2,512,1408]{2,1,0:T(8,128)(2,1)}, f32[2,64,1408]{2,1,0:T(8,128)}, f32[2,64,1408]{2,1,0:T(8,128)}, ...) custom-call(bf16[2,512,1408]{2,1,0:T(8,128)(2,1)S(1)} %get-tuple-ele, ...), custom_call_target="tpu_custom_call" | custom-call | tf_op jit(solution)/shard_map/pallas_call | solution.py:393
  158.2 14.7 %shard_map.189 = (bf16[2,1408,512]{2,1,0:T(8,128)(2,1)S(1)}, f32[2,176,512]{2,1,0:T(8,128)S(1)}, f32[2,176,512]{2,1,0:T(8,128)S(1)}) custom-call(bf16[1,2,1408,512]{3,2,1,0:T(8,128)(2,1)} %refs_0_.3, bf16[2,1408,512]{2,1,0:T(8,128)(2,1)} %refs_1_.3, f32[2,176,512]{2,1,0:T(8,128)} %refs_2_.3, f32[2,176,512]{2,1,0:T(8,128)} %refs_3_.3, ...), custom_call_target="tpu_custom_call" | custom-call | tf_op jit(solution)/shard_map/pallas_call | solution.py:402
  172.9 1.0 shard_map.190

commit v11 on v10

--- a/solution.py
+++ b/solution.py
@@ -199,27 +199,33 @@
             self.finish_sum(p)
             self.step(p)
 
-    def spread(self, hop, done=None):
-        order = [self.live(s, hop) for s in (0, 1)]
+    def spread(self, hop, spare=0):
+        order = [self.live(s, hop + spare) for s in (0, 1)]
         for s in (0, 1):
             if hop == self.far - 1:
                 order[s].sort(key=lambda p, s=s: -self.hops[p][s])
         for pair in zip(*order, strict=True):
             for s, p in enumerate(pair):
-                if done is None:
-                    self.gather_copy(p, s, hop - 1, 0).wait_recv()
-                self.gather_copy(p, s, hop, 1, done).start()
-
-    def gathered(self, hops):
-        for hop in range(1, hops + 1):
+                self.gather_copy(p, s, hop - 1, 0).wait_recv()
+                self.gather_copy(p, s, hop, 1).start()
+
+    def last_hops(self, done):
+        for p in range(self.pieces):
+            for s in (0, 1):
+                self.gather_copy(p, s, self.hops[p][s], 1, done).start()
+
+    def gathered(self, spare):
+        for hop in (self.far - 1, self.far):
             for p in range(self.pieces):
                 for s in (0, 1):
-                    if min(self.hops[p][s], hops) == hop:
-                        self.gather_copy(p, s, hop, 0).wait_recv()
-
-    def all_sent(self, hops, sums):
+                    if self.hops[p][s] == hop:
+                        self.gather_copy(p, s, hop - spare, 0).wait_recv()
+
+    def way_rows(self, spare):
+        return sum((hops[0] - spare) * part[3] for hops, part in zip(self.hops, self.parts, strict=True))
+
+    def all_sent(self, rows):
         for s in (0, 1):
-            rows = sum(self.parts[p][3] for hop in hops for p in self.live(s, hop)) + sums * self.inbox_rows
             whole = self.inbox.at[pl.ds(0, rows)]
             pltpu.make_async_copy(whole, whole, self.send_sem.at[s]).wait()
 
@@ -236,10 +242,6 @@
 
 def behind():
     return lax.rem(lax.axis_index("rep"), 2) == 1
-
-
-def early_hops(n):
-    return n // 2 - 2
 
 
 def early_kernel(n, shape, late_shape, *refs):
@@ -272,16 +274,16 @@
     ring.pass_on()
     ring.take_steps()
     for hop in range(2, ring.far + 1):
-        if hop <= early_hops(n):
-            pl.when(ahead())(functools.partial(late.spread, hop))
+        if hop < ring.far:
+            pl.when(ahead())(functools.partial(late.spread, hop, 1))
         ring.spread(hop)
-    ring.gathered(ring.far)
-    ring.all_sent(range(1, ring.far + 1), True)
-
-    @pl.when(ahead())
-    def _():
-        late.gathered(early_hops(n))
-        late.all_sent(range(1, early_hops(n) + 1), True)
+    ring.gathered(0)
+    ring.all_sent(ring.way_rows(0) + ring.inbox_rows)
+
+    @pl.when(ahead())
+    def _():
+        late.gathered(1)
+        late.all_sent(late.way_rows(1) + late.inbox_rows)
 
 
 def late_kernel(n, shape, *refs):
@@ -291,13 +293,12 @@
     data, done = [take(count) for _ in range(4)], take(count)
     results = [take(count) for _ in range(3)]
     ring = Ring(n, lax.axis_index("dp"), shape, LATE_PIECES, *data, results, take(6), take(4))
-    last = range(early_hops(n) + 1, ring.far + 1)
     ring.greet()
 
     @pl.when(ahead())
     def _():
         pl.delay(HOLD)
-        ring.spread(last[0], done)
+        ring.last_hops(done)
 
     @pl.when(behind())
     def _():
@@ -306,18 +307,29 @@
         ring.load_states()
         ring.pass_on()
         ring.take_steps()
-        for hop in range(2, last[0] + 1):
+        for hop in range(2, ring.far + 1):
             ring.spread(hop)
 
-    for hop in last[1:]:
-        ring.spread(hop)
-    ring.gathered(ring.far)
-    pl.when(ahead())(functools.partial(ring.all_sent, last, False))
-    pl.when(behind())(functools.partial(ring.all_sent, range(1, ring.far + 1), True))
-
-
-def put_early_kernel(n, e, l, *refs):
+    ring.gathered(0)
+    pl.when(ahead())(functools.partial(ring.all_sent, ring.way_rows(0) - ring.way_rows(1)))
+    pl.when(behind())(functools.partial(ring.all_sent, ring.way_rows(0) + ring.inbox_rows))
+
+
+def parted(n, shape, last):
+    weights, _, rows, _ = shape
+    parts, hops, *_ = Ring.cut(n, LATE_PIECES, shape)
+    far, near = n // 2, (n - 1) // 2
+    whole = [far] if last else range(1 - near, near)
+    wanted = [(k, None, 0, rows, away) for k in range(weights) for away in whole]
+    for p, (k, layer, first, count) in enumerate(parts):
+        from_before = (hops[p][0] == far) != last
+        wanted.append((k, layer, first, count, -near if from_before else near))
+    return wanted
+
+
+def put_early_kernel(n, e, shape, *refs):
     refs, sem = list(refs[:-1]), refs[-1]
+    l = shape[0]
     count = 3 * (e + l)
     sources, results = refs[:count], refs[count:]
     early = [pltpu.make_async_copy(sources[i], results[i], sem.at[i]) for i in range(3 * e)]
@@ -326,9 +338,8 @@
 
     @pl.when(ahead())
     def _():
-        reach = early_hops(n)
         late = [pltpu.make_async_copy(sources[i], results[i], sem.at[i]) for i in range(3 * e + l, count)]
-        late += block_copies(n, sources[3 * e : 3 * e + l], results[3 * e : 3 * e + l], range(-reach, reach + 1), sem, count)
+        late += block_copies(n, sources[3 * e : 3 * e + l], results[3 * e : 3 * e + l], parted(n, shape, False), sem, count)
         for copy in late:
             copy.start()
         for copy in late:
@@ -338,24 +349,24 @@
         copy.wait()
 
 
-def block_copies(n, sources, results, aways, sem, first):
+def block_copies(n, sources, results, wanted, sem, first_sem):
     me = lax.axis_index("dp")
     copies = []
-    for source, result in zip(sources, results, strict=True):
-        rows = source.shape[1] // n
-        for away in aways:
-            block = pl.ds(pl.multiple_of(lax.rem(me + (away + n), n) * rows, rows), rows)
-            copies.append(pltpu.make_async_copy(source.at[:, block], result.at[:, block], sem.at[first + len(copies)]))
+    for k, layer, first, count, away in wanted:
+        block_rows = sources[k].shape[1] // n
+        rows = pl.ds(pl.multiple_of(lax.rem(me + (away + n), n) * block_rows + first, ROWS), count)
+        at = (slice(None) if layer is None else layer, rows)
+        copies.append(pltpu.make_async_copy(sources[k].at[at], results[k].at[at], sem.at[first_sem + len(copies)]))
     return copies
 
 
-def put_late_kernel(n, l, *refs):
+def put_late_kernel(n, shape, *refs):
+    l = shape[0]
     sources, results, sem = refs[: 3 * l], refs[6 * l : 9 * l], refs[-1]
 
     @pl.when(ahead())
     def _():
-        reach = early_hops(n)
-        copies = block_copies(n, sources[:l], results[:l], range(reach + 1, n - reach), sem, 3 * l)
+        copies = block_copies(n, sources[:l], results[:l], parted(n, shape, True), sem, 3 * l)
         for copy in copies:
             copy.start()
         for copy in copies:
@@ -391,11 +402,11 @@
             compiler_params=pltpu.CompilerParams(collective_id=0, has_side_effects=True, vmem_limit_bytes=GRANT_EARLY),
         )(*g[early], *w[early], *m[early], *v[early], *g[late], *w[late], *m[late], *v[late])
         first = pl.pallas_call(
-            functools.partial(put_early_kernel, n, e, l),
+            functools.partial(put_early_kernel, n, e, late_shape),
             out_shape=hbm((*early_results, *late_results)),
             in_specs=[VMEM] * (3 * (e + l)),
             out_specs=[HBM] * (3 * (e + l)),
-            scratch_shapes=[DMA((3 * (e + l) + l * (2 * early_hops(n) + 1),))],
+            scratch_shapes=[DMA((3 * (e + l) + len(parted(n, late_shape, False)),))],
             compiler_params=pltpu.CompilerParams(vmem_limit_bytes=1 << 20),
         )(*first)
         first, half = first[: 3 * e], first[3 * e :]
@@ -408,11 +419,11 @@
             compiler_params=pltpu.CompilerParams(collective_id=1, has_side_effects=True, vmem_limit_bytes=GRANT_LATE),
         )(*g[late], *w[late], *m[late], *v[late], *half[:l])
         second = pl.pallas_call(
-            functools.partial(put_late_kernel, n, l),
+            functools.partial(put_late_kernel, n, late_shape),
             out_shape=hbm(late_results),
             in_specs=[VMEM] * (3 * l) + [HBM] * (3 * l),
             out_specs=[HBM] * (3 * l),
-            scratch_shapes=[DMA((3 * l + l * (n - 1 - 2 * early_hops(n)),))],
+            scratch_shapes=[DMA((3 * l + len(parted(n, late_shape, True)),))],
             input_output_aliases={3 * l + i: i for i in range(3 * l)},
             compiler_params=pltpu.CompilerParams(vmem_limit_bytes=1 << 20),
         )(*second, *half)

time: 174 us -> 175 us (level)
  Pallas kernels: 173 us -> 175 us
    pallas_call x1, Pallas kernels: 153 us -> 157 us  [step(): pl.pallas_call(functools.partial(early_kernel, n, early_shape, late_shape...]
    pallas_call x1, Pallas kernels: 14.7 us -> 12.3 us  [step(): pl.pallas_call(functools.partial(late_kernel, n, late_shape), out_shape=v...]
where the time goes in v11:
time: 175 us
  Pallas kernels  175 us (100%)
    pallas_call x1, Pallas kernels, step(): pl.pallas_call(functools.partial(early_kernel, n, early_shape, late_shape...  157 us
    pallas_call x1, Pallas kernels, step(): pl.pallas_call(functools.partial(late_kernel, n, late_shape), out_shape=v...  12.3 us
    pallas_call x1, Pallas kernels, step(): pl.pallas_call(functools.partial(put_early_kernel, n, e, late_shape), out...  4.63 us

profile of v11, /device:TPU:22, one launch (start us, length us, event | category | flops | bytes accessed | tf_op | source)
XLA Modules:
  0.0 175.4 jit_solution(12782931176506425279)
XLA Ops:
  0.6 156.8 %shard_map.187 = (bf16[2,512,1408]{2,1,0:T(8,128)(2,1)S(1)}, bf16[2,512,1408]{2,1,0:T(8,128)(2,1)S(1)}, f32[2,64,1408]{2,1,0:T(8,128)S(1)}, f32[2,64,1408]{2,1,0...) custom-call(bf16[1,2,512,1408]{3,2,1,0:T(8,128)(2,1)} %refs_0_.2, ...), custom_call_target="tpu_custom_call" | custom-call | tf_op jit(solution)/shard_map/pallas_call | solution.py:396
  157.5 4.6 %shard_map.188 = (bf16[2,512,1408]{2,1,0:T(8,128)(2,1)}, bf16[2,512,1408]{2,1,0:T(8,128)(2,1)}, f32[2,64,1408]{2,1,0:T(8,128)}, f32[2,64,1408]{2,1,0:T(8,128)}, ...) custom-call(bf16[2,512,1408]{2,1,0:T(8,128)(2,1)S(1)} %get-tuple-ele, ...), custom_call_target="tpu_custom_call" | custom-call | tf_op jit(solution)/shard_map/pallas_call | solution.py:404
  162.1 12.3 %shard_map.189 = (bf16[2,1408,512]{2,1,0:T(8,128)(2,1)S(1)}, f32[2,176,512]{2,1,0:T(8,128)S(1)}, f32[2,176,512]{2,1,0:T(8,128)S(1)}) custom-call(bf16[1,2,1408,512]{3,2,1,0:T(8,128)(2,1)} %refs_0_.3, bf16[2,1408,512]{2,1,0:T(8,128)(2,1)} %refs_1_.3, f32[2,176,512]{2,1,0:T(8,128)} %refs_2_.3, f32[2,176,512]{2,1,0:T(8,128)} %refs_3_.3, ...), custom_call_target="tpu_custom_call" | custom-call | tf_op jit(solution)/shard_map/pallas_call | solution.py:413
  174.4 0.9 shard_map.190

commit v12 on v11

--- a/solution.py
+++ b/solution.py
@@ -11,8 +11,8 @@
 DMA = pltpu.SemaphoreType.DMA
 HBM, VMEM = pl.BlockSpec(memory_space=pltpu.HBM), pl.BlockSpec(memory_space=pltpu.VMEM)
 ROWS = 16
-EARLY_PIECES, LATE_PIECES = 1, 2
-HOLD = 3200
+EARLY_PIECES, LATE_PIECES = 1, 4
+HOLD = 900
 GRANT_EARLY, GRANT_LATE = 54_000_000, 61_500_000
 
 

time: 175 us -> 174 us (level)
  Pallas kernels: 175 us -> 173 us
where the time goes in v12:
time: 174 us
  Pallas kernels  173 us (99%)
    pallas_call x1, Pallas kernels, step(): pl.pallas_call(functools.partial(early_kernel, n, early_shape, late_shape...  157 us
    pallas_call x1, Pallas kernels, step(): pl.pallas_call(functools.partial(late_kernel, n, late_shape), out_shape=v...  11 us
    pallas_call x1, Pallas kernels, step(): pl.pallas_call(functools.partial(put_early_kernel, n, e, late_shape), out...  4.66 us

profile of v12, /device:TPU:22, one launch (start us, length us, event | category | flops | bytes accessed | tf_op | source)
XLA Modules:
  0.0 173.9 jit_solution(2102052693337365135)
XLA Ops:
  0.6 156.6 %shard_map.187 = (bf16[2,512,1408]{2,1,0:T(8,128)(2,1)S(1)}, bf16[2,512,1408]{2,1,0:T(8,128)(2,1)S(1)}, f32[2,64,1408]{2,1,0:T(8,128)S(1)}, f32[2,64,1408]{2,1,0...) custom-call(bf16[1,2,512,1408]{3,2,1,0:T(8,128)(2,1)} %refs_0_.2, ...), custom_call_target="tpu_custom_call" | custom-call | tf_op jit(solution)/shard_map/pallas_call | solution.py:396
  157.2 4.7 %shard_map.188 = (bf16[2,512,1408]{2,1,0:T(8,128)(2,1)}, bf16[2,512,1408]{2,1,0:T(8,128)(2,1)}, f32[2,64,1408]{2,1,0:T(8,128)}, f32[2,64,1408]{2,1,0:T(8,128)}, ...) custom-call(bf16[2,512,1408]{2,1,0:T(8,128)(2,1)S(1)} %get-tuple-ele, ...), custom_call_target="tpu_custom_call" | custom-call | tf_op jit(solution)/shard_map/pallas_call | solution.py:404
  161.9 11.0 %shard_map.189 = (bf16[2,1408,512]{2,1,0:T(8,128)(2,1)S(1)}, f32[2,176,512]{2,1,0:T(8,128)S(1)}, f32[2,176,512]{2,1,0:T(8,128)S(1)}) custom-call(bf16[1,2,1408,512]{3,2,1,0:T(8,128)(2,1)} %refs_0_.3, bf16[2,1408,512]{2,1,0:T(8,128)(2,1)} %refs_1_.3, f32[2,176,512]{2,1,0:T(8,128)} %refs_2_.3, f32[2,176,512]{2,1,0:T(8,128)} %refs_3_.3, ...), custom_call_target="tpu_custom_call" | custom-call | tf_op jit(solution)/shard_map/pallas_call | solution.py:413
  172.9 1.0 shard_map.190
